TPU v7x, 32 devices: a whole 2x2x4 slice. The times are simulated.
32 devices in a mesh: fsdp: 8 (over z, y), tensor: 4 (over x, core).
Axes of the slice: x: 2, y: 2, z: 4, core: 2. Of those that a mesh axis runs over, the one named last changes fastest.
Arguments:
- tokens: bfloat16 [12288, 768], P(('fsdp', 'tensor')), may hold values from -6 to 6
- attn_weight: bfloat16 [3, 768, 768], P(None, 'fsdp', 'tensor'), may hold values from -0.21875 to 0.21875
- query_value_bias: bfloat16 [2, 12, 64], P(None, 'tensor', 'fsdp'), may hold values from -3 to 3
- out_weight: bfloat16 [768, 768], P('tensor', 'fsdp'), may hold values from -1.25 to 1.25
- hidden_weight: bfloat16 [768, 3072], P('fsdp', 'tensor'), may hold values from -0.21875 to 0.21875
- hidden_bias: bfloat16 [48, 64], P('tensor', 'fsdp'), may hold values from -3 to 3
- down_weight: bfloat16 [3072, 768], P('tensor', 'fsdp'), may hold values from -0.109375 to 0.109375
- norm_gains: bfloat16 [2, 768], P(None, 'fsdp'), may hold values from 0.5 to 1.5
- norm_biases: bfloat16 [2, 768], P(None, 'fsdp'), may hold values from -2 to 2
- output_biases: bfloat16 [2, 768], P(None, 'fsdp'), may hold values from -2 to 2
- segment_ids: int32 [12288], P('fsdp'), may hold values from 0 to 15, as said below
- padding: int32 [12288], P('fsdp'), may hold values from 0 to 1, as said below
- cotangent: bfloat16 [12288, 768], P(('fsdp', 'tensor')), may hold values from -6 to 6
Outputs:
- layer_out: bfloat16 [12288, 768], P(('fsdp', 'tensor'))
- tokens_grad: float32 [12288, 768], P(('fsdp', 'tensor'))
- attn_weight_grad: float32 [3, 768, 768], P(None, 'fsdp', 'tensor')
- query_value_bias_grad: float32 [2, 12, 64], P(None, 'tensor', 'fsdp')
- out_weight_grad: float32 [768, 768], P('tensor', 'fsdp')
- hidden_weight_grad: float32 [768, 3072], P('fsdp', 'tensor')
- hidden_bias_grad: float32 [48, 64], P('tensor', 'fsdp')
- down_weight_grad: float32 [3072, 768], P('tensor', 'fsdp')
- norm_gains_grad: float32 [2, 768], P(None, 'fsdp')
- norm_biases_grad: float32 [2, 768], P(None, 'fsdp')
- output_biases_grad: float32 [2, 768], P(None, 'fsdp')
- root_squares: float32 [3], replicated
Inputs may be any that keep to these rules, and one draw needn't show every extreme that they name: `segment_ids`: within each sequence of 1536 positions, segment ids start at 0 and rise by one at each new document; every document has 96 to 768 tokens except the last of a sequence, which its end may cut; some document has exactly 768 tokens. Within each sequence, the padding positions (value 0) form a tail of at most 192 positions.
All inputs are finite; a program needn't handle non-finite values.
Results may differ from a plain program's by a relative error of at most 0.013.
The roundings to bfloat16 on the way count: a program that leaves them out, or rounds other values in their place, can miss the bound.
Values may be sent and summed in bfloat16 or wider, within the bound.
A program may use at most 192 MiB of HBM per device.

v0:
```python
import functools

import jax
import jax.numpy as jnp
from jax import lax
from jax.experimental import pallas as pl
from jax.experimental.pallas import tpu as pltpu
from jax.sharding import PartitionSpec as P

DH = 64
EPSILON = 1e-12
BQ = 256
BK = 256
F32 = jnp.float32
BF = jnp.bfloat16
MESH = pl.DeviceIdType.MESH
DMA = pltpu.SemaphoreType.DMA
ROWS = 128
MISC = 16
MOST = 768


def places(n):
    t = lax.axis_index("tensor")
    f = lax.axis_index("fsdp")
    c, x = t % 2, t // 2
    core, cross, diag = 2 * x + 1 - c, 2 * (1 - x) + c, 2 * (1 - x) + 1 - c
    y, z = f % 2, f // 2
    place = z + y * (n - 1 - 2 * z)

    def at(p):
        y = p // max(n // 2, 1)
        return 2 * (p + y * (n - 1 - 2 * p)) + y

    return t, f, core, cross, diag, place, at


def send(src, dst, ss, rs, **axes):
    return pltpu.make_async_remote_copy(
        src_ref=src, dst_ref=dst, send_sem=ss, recv_sem=rs, device_id=axes, device_id_type=MESH
    )


def meet(core, cross, ring, *more):
    gate = pltpu.get_barrier_semaphore()
    for where in (core, cross) + more:
        pl.semaphore_signal(gate, inc=1, device_id={"tensor": where}, device_id_type=MESH)
    for where in ring:
        pl.semaphore_signal(gate, inc=1, device_id={"fsdp": where}, device_id_type=MESH)
    pl.semaphore_wait(gate, 2 + len(ring) + len(more))


def both_ways(n, place, at, local, held, sems):
    rs, rr, ls, lr = sems
    nxt, prv = at((place + 1) % n), at((place + n - 1) % n)
    far = n // 2
    half = local.shape[0] // 2
    steps = []
    for s in range(far):
        a, b = at((place - s + n) % n), at((place + s) % n)
        up = local if s == 0 else held.at[a]
        down = local if s == 0 else held.at[b]
        row = []
        for k in (0, 1):
            part = pl.ds(k * half, half)
            if s < far - 1 or k == 0:
                row.append(send(up.at[part], held.at[a, part], rs.at[s, k], rr.at[s, k], fsdp=nxt))
            if s < far - 1 or k == 1:
                row.append(send(down.at[part], held.at[b, part], ls.at[s, k], lr.at[s, k], fsdp=prv))
        steps.append(row)
    return steps


def ring_on(steps, s):
    for i, c in enumerate(steps[s]):
        if s < len(steps) - 1:
            steps[s - 1][i].wait_recv()
            c.start()
    if s == len(steps) - 1:
        steps[s - 1][0].wait_recv()
        steps[s][0].start()
        steps[s - 1][1].wait_recv()
        steps[s - 1][2].wait_recv()
        steps[s - 1][3].wait_recv()
        steps[s][1].start()


def ring_end(steps):
    for c in steps[-1]:
        c.wait_recv()
    for row in steps:
        for c in row:
            c.wait_send()


def mm(a, b, ca=1, cb=0):
    return lax.dot_general(a, b, (((ca,), (cb,)), ((), ())), preferred_element_type=F32)


def some(ref, rows, c0, c1, j, count):
    g = ref.shape[0]
    if g % count:
        size = rows // count
        return ref[0, j * size : (j + 1) * size, c0:c1]
    g //= count
    return ref[j * g : (j + 1) * g, :rows, c0:c1].reshape(g * rows, c1 - c0)


def whole(ref, rows, c0, c1):
    g = ref.shape[0]
    return ref[:, :rows, c0:c1].reshape(g * rows, c1 - c0)


def fold_max(s):
    return jnp.max(s.reshape(s.shape[0] // 8, 8, s.shape[1]), axis=0)


def fold_sum(s):
    return jnp.sum(s.reshape(s.shape[0] // 8, 8, s.shape[1]), axis=0)


def col_sum(s):
    return jnp.sum(fold_sum(s), axis=0, keepdims=True)


def project_kernel(n, ring, *refs):
    refs = list(refs)
    pop = lambda m: [refs.pop(0) for _ in range(m)]
    tok, seg, alive = pop(3)
    if ring:
        far = [seg, alive] + pop(7)
    else:
        (wg,) = pop(1)
    full, qkv, misc, sq, sk, live, lives, bounds = pop(8)
    if ring:
        wg, mine = pop(2)
        near = pop(len(far))
        nsem = pop(1)[0]
        for j in range(len(far)):
            pltpu.make_async_copy(far[j], near[j], nsem.at[j]).start()
    lsem, xs, xr, cs, cr, fs, fr = pop(7)
    gsems = refs
    t, f, core, cross, diag, place, at = places(n)
    rows, d = tok.shape
    part = wg.shape[1] - MISC
    head = qkv.shape[2]
    if ring:
        for j in range(len(far)):
            pltpu.make_async_copy(far[j], near[j], nsem.at[j]).wait()
        seg, alive, aw, ow, gains, shifts, biases, hb, qvb = near
        mine[:part] = jnp.concatenate([aw[0], aw[1], aw[2], ow[...].astype(F32).T.astype(BF)], axis=1)
        col = lax.broadcasted_iota(jnp.int32, (part, d), 1)
        row = lax.broadcasted_iota(jnp.int32, (part, d), 0)
        spread = (col == f * part + row).astype(BF)
        wide = [mm(r[...], spread) for r in (gains, shifts, biases)]
        k = hb.shape[0]
        col = lax.broadcasted_iota(jnp.int32, (k, d), 1)
        row = lax.broadcasted_iota(jnp.int32, (k, d), 0)
        spread = (col % DH == f * k + row).astype(BF)
        h = mm(hb[...].astype(F32).T.astype(BF), spread)
        col = lax.broadcasted_iota(jnp.int32, h.shape, 1) // DH
        row = lax.broadcasted_iota(jnp.int32, h.shape, 0)
        h = jnp.sum(jnp.where(col == row, h, 0.0), axis=0, keepdims=True)
        b = jnp.zeros((1, d), F32)
        col = lax.broadcasted_iota(jnp.int32, (1, d), 1) // DH
        heads = qvb.shape[0]
        for j in range(heads):
            x = mm(qvb[j], spread)
            b = jnp.where(col == j, x[0:1], jnp.where(col == 2 * heads + j, x[1:2], b))
        mine[part:] = jnp.concatenate(wide + [h, b, jnp.zeros((8, d), F32)], axis=0).astype(BF)
        steps = both_ways(n, place, at, mine, wg, gsems)
        meet(core, cross, (at((place + 1) % n), at((place + n - 1) % n)))
    else:
        meet(core, cross, ())
    R = range(rows // ROWS)
    cut = lambda i: pl.ds(i * ROWS, ROWS)
    xc = [send(tok.at[cut(i)], full.at[t, cut(i)], xs.at[i], xr.at[i], tensor=cross) for i in R]
    cc = [send(tok.at[cut(i)], full.at[t, cut(i)], cs.at[i], cr.at[i], tensor=core) for i in R]
    fc = [send(full.at[cross, cut(i)], full.at[cross, cut(i)], fs.at[i], fr.at[i], tensor=core) for i in R]
    own = [pltpu.make_async_copy(tok, full.at[t], lsem.at[0])]
    if ring:
        own.append(pltpu.make_async_copy(mine, wg.at[f], lsem.at[1]))
        for c in steps[0]:
            c.start()
    for c in xc + cc + own:
        c.start()

    groups = seg.shape[0]
    ids = seg[...].astype(F32)
    on = alive[...]
    keys = jnp.where(on == 1, ids, -1.0)
    onf = on.astype(F32)
    for g in range(groups):
        c = slice(g * 128, (g + 1) * 128)
        sq[:, c] = ids[g : g + 1]
        live[:, c] = onf[g : g + 1]
        sk[c, :] = jnp.broadcast_to(keys[g : g + 1], (128, 128)).T
        lives[c, :] = jnp.broadcast_to(onf[g : g + 1], (128, 128)).T
    per = BQ // 128
    for i in range(groups // per):
        under = jnp.sum((ids < ids[i * per : i * per + 1, 0:1]).astype(F32))
        upto = jnp.sum((ids <= ids[(i + 1) * per - 1 : (i + 1) * per, 127:128]).astype(F32))
        bounds[2 * i] = under.astype(jnp.int32) // BK
        bounds[2 * i + 1] = (upto.astype(jnp.int32) + BK - 1) // BK

    if ring:
        for s in range(1, len(steps)):
            ring_on(steps, s)
    for i in R:
        xc[i].wait_recv()
        fc[i].start()
    for c in own:
        c.wait()
    for c in cc:
        c.wait_recv()
    if ring:
        ring_end(steps)
    misc[...] = jnp.sum(wg[:, part:, :].astype(F32), axis=0)
    w = 3 * head

    def block(i):
        p = mm(full[i], whole(wg, part, 0, w)) + misc[7:8, :w]
        for j in range(3):
            qkv[j, pl.ds(i * rows, rows), :] = p[:, j * head : (j + 1) * head].astype(BF)

    def three(j, _):
        block(lax.select(j == 0, t, lax.select(j == 1, core, cross)))
        return 0

    lax.fori_loop(0, 3, three, 0)
    for c in fc:
        c.wait_recv()
    block(diag)
    for c in xc + cc + fc:
        c.wait_send()


def project(n, tok, head, seg, alive, raw=None, wg=None):
    ring = wg is None
    vm = pl.BlockSpec(memory_space=pltpu.VMEM)
    rows, d = tok.shape
    nch = rows // ROWS
    s = jax.ShapeDtypeStruct
    total = 4 * rows
    outs = [
        s((4, rows, d), BF),
        s((3, total, head), BF),
        s((MISC, d), F32),
        s((1, total), F32),
        s((total, 128), F32),
        s((1, total), F32),
        s((total, 128), F32),
        s((2 * total // BQ,), jnp.int32),
    ]
    specs = [vm] * 7 + [pl.BlockSpec(memory_space=pltpu.SMEM)]
    scratch = [DMA((2,))] + [DMA((nch,))] * 6
    ops = (tok, seg.reshape(-1, 128), alive.reshape(-1, 128))
    if ring:
        ops = tuple(pltpu.with_memory_space_constraint(x, pltpu.HBM) for x in ops + raw)
        outs.append(s((n, d // n + MISC, d), BF))
        specs.append(vm)
        held = [pltpu.VMEM(x.shape, x.dtype) for x in ops[1:]]
        scratch = [pltpu.VMEM((d // n + MISC, d), BF)] + held + [DMA((len(held),))] + scratch + [DMA((n // 2, 2))] * 4
    else:
        ops += (wg,)
    got = pl.pallas_call(
        functools.partial(project_kernel, n, ring),
        in_specs=[pl.BlockSpec(memory_space=pltpu.HBM) if ring else vm] * len(ops),
        out_specs=specs,
        out_shape=outs,
        scratch_shapes=scratch,
        compiler_params=pltpu.CompilerParams(
            collective_id=1, has_side_effects=True, vmem_limit_bytes=2 << 20
        ),
        name="project",
    )(*ops)
    return tuple(got) if ring else tuple(got) + (wg,)


def moments(h):
    mean = jnp.mean(h, axis=-1, keepdims=True)
    c = h - mean
    r = lax.rsqrt(jnp.mean(c * c, axis=-1, keepdims=True) + EPSILON)
    return c * r, r


def norm_back(dy, g, xhat, r):
    dx = dy * g
    return r * (
        dx
        - jnp.mean(dx, axis=-1, keepdims=True)
        - xhat * jnp.mean(dx * xhat, axis=-1, keepdims=True)
    )


def scatter_tools(core, cross, part, cs, cr, xs, xr, sems):
    ccs, ccr, xxs, xxr = sems
    a = lambda i, k: send(cs.at[k], cr.at[k], ccs.at[i, k], ccr.at[i, k], tensor=core)
    b = lambda i, k: send(xs.at[k], xr.at[k], xxs.at[i, k], xxr.at[i, k], tensor=cross)

    def put(i, k, tile, count):
        if i > 0:
            a(i - 1, k).wait_send()
        width = part.shape[-1] // count
        for j in range(count):
            p = tile(j)
            m = p.shape[0] // 4
            c = slice(j * width, (j + 1) * width)
            cs[k, 0, :, c] = p[m : 2 * m].astype(BF)
            cs[k, 1, :, c] = p[3 * m :].astype(BF)
            part[k, 0, :, c] = p[:m]
            part[k, 1, :, c] = p[2 * m : 3 * m]
        a(i, k).start()

    def across(i, k):
        a(i, k).wait_recv()
        if i > 0:
            b(i - 1, k).wait_send()
        xs[k] = (part[k, 1] + cr[k, 1].astype(F32)).astype(BF)
        b(i, k).start()
        part[k, 0] = part[k, 0] + cr[k, 0].astype(F32)

    def take(i, k):
        b(i, k).wait_recv()
        return part[k, 0] + xr[k].astype(F32)

    def end(i, k):
        a(i, k).wait_send()
        b(i, k).wait_send()

    return put, across, take, end


def block_rows(ref, device, c0, c1, n):
    size = ref.shape[0] // n
    return ref.at[pl.ds(pl.multiple_of(device * size, size), size), pl.ds(c0, c1 - c0)]


class RingSum:
    def __init__(self, n, place, at, local, c0, c1, rbuf, ss, rs, right):
        self.n, self.rbuf = n, rbuf
        target = at((place + 1) % n) if right else at((place + n - 1) % n)
        step = -1 if right else 1
        self.own = lambda s: block_rows(local, at((place + step * (1 + s) + 2 * n) % n), c0, c1, n)

        def copy(s):
            src = self.own(0) if s == 0 else rbuf.at[s - 1]
            return send(src, rbuf.at[s], ss.at[s], rs.at[s], fsdp=target)

        self.copy = copy

    def go(self, s):
        if s > 0:
            self.copy(s - 1).wait_recv()
            self.rbuf[s - 1] = (self.rbuf[s - 1].astype(F32) + self.own(s)[...].astype(F32)).astype(BF)
        self.copy(s).start()

    def close(self):
        s = self.n - 2
        self.copy(s).wait_recv()
        return self.rbuf[s].astype(F32) + self.own(s + 1)[...].astype(F32)

    def sent(self):
        for s in range(self.n - 1):
            self.copy(s).wait_send()


def ring_group(n, place, at, local, tracks):
    m = len(tracks)
    q = [RingSum(n, place, at, local, j * 128, j * 128 + 128, *tracks[j], j < m // 2) for j in range(m)]
    left = list(range(n - 1))

    def go():
        if left:
            s = left.pop(0)
            for j in range(m // 2):
                q[j].go(s)
                q[j + m // 2].go(s)

    def close():
        while left:
            go()
        x = jnp.concatenate([r.close() for r in q], axis=1)
        for r in q:
            r.sent()
        return x

    return go, close


def ring_scratch(n, rows, widths):
    out = []
    for w in widths:
        out += [pltpu.VMEM((n - 1, rows, w), BF)]
        out += [DMA((n - 1,)), DMA((n - 1,))]
    return out


def attend_block(i, lo, hi, heads, sq_ref, sk_ref, pad_ref, qt, kh, vt, sc, ctx_ref, octx_ref, lse_ref):
    q0 = pl.multiple_of(i * BQ, BQ)
    sq = sq_ref[0:1, pl.ds(q0, BQ)]
    qpos = q0 + lax.broadcasted_iota(jnp.int32, (BK, BQ), 1)
    part = sc.shape[1] // BK
    spot = lambda h, j: (sc.shape[0] // heads * h + j // part, pl.ds(pl.multiple_of(j % part * BK, BK), BK), slice(None))

    def first(j, c):
        k0 = pl.multiple_of(j * BK, BK)
        sk = jnp.concatenate([sk_ref[pl.ds(k0, BK), :]] * (BQ // 128), axis=1)
        kpos = k0 + lax.broadcasted_iota(jnp.int32, (BK, BQ), 0)
        ok = (sk == sq) | (kpos == qpos)
        out = []
        for h in range(heads):
            s = jnp.where(ok, mm(kh(h, j)[...], qt(h, i)[...]), -1e30)
            sc[spot(h, j)] = s
            out.append(jnp.maximum(c[h], fold_max(s)))
        return tuple(out)

    m = lax.fori_loop(lo, hi, first, (jnp.full((8, BQ), -3e38, F32),) * heads)
    m = [jnp.max(x, axis=0, keepdims=True) for x in m]

    def second(j, c):
        out = []
        for h in range(heads):
            l, acc = c[2 * h : 2 * h + 2]
            p = jnp.exp(sc[spot(h, j)] - m[h])
            out += [l + fold_sum(p), acc + mm(vt(h, j)[...], p.astype(BF))]
        return tuple(out)

    c = lax.fori_loop(lo, hi, second, (jnp.zeros((8, BQ), F32), jnp.zeros((DH, BQ), F32)) * heads)
    o = []
    for h in range(heads):
        l, acc = c[2 * h : 2 * h + 2]
        l = jnp.sum(l, axis=0, keepdims=True)
        lse_ref[h : h + 1, pl.ds(q0, BQ)] = m[h] + jnp.log(l)
        o.append(acc / l)
    ot = jnp.concatenate(o, axis=0) * pad_ref[0:1, pl.ds(q0, BQ)]
    octx_ref[:, pl.ds(q0, BQ)] = ot
    ctx_ref[pl.ds(q0, BQ), :] = ot.T.astype(BF)


def middle_kernel(n, ring, *refs):
    refs = list(refs)
    pop = lambda m: [refs.pop(0) for _ in range(m)]
    qkv, sq, sk, live_row, wg, misc, full, cot_hbm, pad = pop(9)
    if ring:
        wh, wd = pop(2)
    else:
        (wf,) = pop(1)
    out, dfirst, dctx, octx, lse, gout, gup, odown, sums = pop(9)
    gdown = odown
    if ring:
        (wf, gdown) = pop(2)
    ctx, call, slab, wo, dsend = pop(5)
    (norm, dff, acted, dgelu, pre, dpre, first, xhat, r1, part, csem, lsem) = pop(12)
    cs, cr, xs, xr = pop(4)
    ocs, ocr, oxs, oxr = pop(4)
    rsem = pop(4)
    gsem = pop(6)
    osem = pop(4)
    ssem = pop(6)
    asem = pop(6)
    dsem = pop(6)
    ff = wf.shape[2] // 2
    if ring:
        wsem = pop(4)
        tracks = [pop(3) for _ in range(ff // 128)]
    t, f, core, cross, diag, place, at = places(n)
    rows, d = out.shape
    fetch = pltpu.make_async_copy(cot_hbm, out, csem.at[0])
    fetch.start()
    nch = rows // ROWS
    wpart = wg.shape[1] - MISC
    fpart = wf.shape[1]
    width = ctx.shape[1]
    heads = width // DH
    where = (t, core, cross, diag)
    put, across, take, end = scatter_tools(core, cross, part, cs, cr, xs, xr, rsem)
    gs = {}
    for i, buf in enumerate((norm, dff)):
        gs[i] = (
            lambda k, buf=buf, i=i: send(buf.at[k, 0], buf.at[k, 2], gsem[0].at[i, k], gsem[1].at[i, k], tensor=cross),
            lambda k, buf=buf, i=i: send(buf.at[k, 0], buf.at[k, 1], gsem[2].at[i, k], gsem[3].at[i, k], tensor=core),
            lambda k, buf=buf, i=i: send(buf.at[k, 2], buf.at[k, 3], gsem[4].at[i, k], gsem[5].at[i, k], tensor=core),
        )

    def share(i, k):
        gs[i][0](k).start()
        gs[i][1](k).start()

    def shared(i, k):
        gs[i][0](k).wait_recv()
        gs[i][2](k).start()
        gs[i][1](k).wait_recv()
        gs[i][2](k).wait_recv()

    lane0 = d - slab.shape[-1]
    mine = wg.at[:, pl.ds(0, wpart), pl.ds(lane0, slab.shape[-1])]
    slabs = (
        send(mine, slab.at[1], ssem[0].at[0], ssem[1].at[0], tensor=cross),
        send(mine, slab.at[0], ssem[2].at[0], ssem[3].at[0], tensor=core),
        send(slab.at[1], slab.at[2], ssem[4].at[0], ssem[5].at[0], tensor=core),
    )

    def rows_at(w, k):
        return pl.ds(pl.multiple_of(w * rows + k * ROWS, ROWS), ROWS)

    def give(j, k):
        return send(ctx.at[rows_at(where[j], k), :], call.at[k, j], asem[2 * j - 2].at[k], asem[2 * j - 1].at[k], tensor=where[j])

    def back(j, k):
        return send(dsend.at[k, j - 1], dctx.at[rows_at(t, k), :], dsem[2 * j - 2].at[k], dsem[2 * j - 1].at[k], tensor=where[j])

    if ring:
        load = [
            pltpu.make_async_copy(wh, wf.at[f, :, pl.ds(0, ff)], lsem.at[0]),
            pltpu.make_async_copy(wd, wf.at[f, :, pl.ds(ff, ff)], lsem.at[1]),
        ]
        for c in load:
            c.start()
        for c in load:
            c.wait()
        steps = both_ways(n, place, at, wf.at[f], wf, wsem)
        meet(core, cross, (at((place + 1) % n), at((place + n - 1) % n)), diag)
        for c in steps[0]:
            c.start()
    else:
        meet(core, cross, (), diag)
    slabs[0].start()
    slabs[1].start()
    sums[...] = jnp.zeros_like(sums)

    blocks = 4 * rows // BQ
    across_lanes = d // BQ

    def turned(top):
        def tile(h, i):
            lanes = pl.ds(pl.multiple_of(i % across_lanes * BQ, BQ), BQ)
            return dff.at[h, i // across_lanes, pl.ds(top, DH), lanes]

        return tile

    qt, vt = turned(0), turned(DH)
    stack = 4 * ROWS // BK

    def kh(h, j):
        lanes = pl.ds(pl.multiple_of(j // stack * 128, 128), DH)
        return acted.at[h, pl.ds(pl.multiple_of(j % stack * BK, BK), BK), lanes]

    def prepare(i, _):
        r = pl.ds(pl.multiple_of(i * BQ, BQ), BQ)
        qs = (qkv[0, r, :].astype(F32) * 0.125).T.astype(BF)
        vs = qkv[2, r, :].astype(F32).T.astype(BF)
        ks = qkv[1, r, :]
        for h in range(heads):
            c = slice(h * DH, (h + 1) * DH)
            qt(h, i)[...] = qs[c]
            vt(h, i)[...] = vs[c]
            kh(h, i)[...] = ks[:, c]
        return 0

    lax.fori_loop(0, blocks, prepare, 0)
    reach = (MOST - 2 + BK) // BK

    def attend(base, stride, count):
        def body(i, _):
            b = base + i * stride
            lo = jnp.maximum(b - reach, 0)
            hi = jnp.minimum(b + reach + 1, blocks)
            attend_block(b, lo, hi, heads, sq, sk, live_row, qt, kh, vt, dgelu, ctx, octx, lse)
            return 0

        lax.fori_loop(0, count, body, 0)

    def give_when(sent):
        for w in range(4):
            ks = [k for k in range(nch) if k in sent[w]]
            for j in (3, 2, 1):

                @pl.when(where[j] == w)
                def _(j=j, ks=ks):
                    for k in ks:
                        give(j, k).start()

    def rows_of(k):
        return pl.ds(pl.multiple_of(k * ROWS, ROWS), ROWS)

    def pad_rows(k):
        return pad[rows_at(t, k), 0:1]

    def live(k, x):
        s = jnp.sum(x * x, axis=-1, keepdims=True) * pad_rows(k)
        return jnp.sum(s, axis=0, keepdims=True)

    lane = lax.broadcasted_iota(jnp.int32, (1, d), 1)

    def note(j, v):
        sums[7:8, :] += jnp.where(lane == d // 2 + j, v, 0.0)

    def norm_one(k):
        for j in (1, 2, 3):
            give(j, k).wait_recv()
        call[k, 0] = ctx[rows_at(t, k), :]
        x = full[t, rows_of(k), :].astype(F32)
        branch = misc[4:5, :]
        for j in range(4):
            branch = branch + mm(call[k, j], wo[j], 1, 1)
        xh, r = moments(x + branch)
        y = xh * misc[0:1, :] + misc[2:3, :]
        first[k] = y
        xhat[k] = xh
        r1[k] = r
        norm[k, 0] = y.astype(BF)
        share(0, k)
        note(0, live(k, x))
        note(1, live(k, branch))
        note(3, jnp.sum(pad_rows(k), axis=0, keepdims=True))

    def loop(fn):
        def body(k, _):
            fn(k)
            return 0

        lax.fori_loop(0, nch, body, 0)

    done, whole_rows = set(), [set() for _ in range(4)]

    def ran(ids):
        done.update(r for b in ids for r in range(b * BQ // ROWS, (b + 1) * BQ // ROWS))
        fresh = [
            {k for k in range(nch) if w * nch + k in done and k not in whole_rows[w]} for w in range(4)
        ]
        for w in range(4):
            whole_rows[w] |= fresh[w]
        give_when(fresh)

    attend(0, 1, 2)
    ran((0, 1))
    if ring:
        ring_on(steps, 1)
    attend(3, 1, 2)
    ran((3, 4))
    slabs[0].wait_recv()
    slabs[2].start()
    if ring:
        ring_on(steps, 2)
    attend(2, 1, 1)
    slabs[1].wait_recv()
    slabs[2].wait_recv()
    wo[0] = whole(wg, wpart, lane0, d)[:, -width:]
    for j in range(3):
        wo[j + 1] = slab[j].reshape(d, slab.shape[-1])[:, -width:]
    norm_one(0)
    attend(5, 1, 1)
    ran((2, 5))
    if ring:
        for s in range(3, len(steps)):
            ring_on(steps, s)
    for k in range(1, nch):
        norm_one(k)
    if ring:
        ring_end(steps)
    inv = 0.7071067811865476
    thirds = ff // BQ

    def feed(k):
        shared(0, k)
        def half(b):
            x = norm[k, 2 * b : 2 * b + 2].reshape(2 * ROWS, d)
            for c in range(0, ff, 256):
                pre[:, c : c + 256] = mm(x, whole(wf, fpart, c, c + 256)) + misc[6:7, c : c + 256]

        def act(i, b):
            u = pre[pl.ds(pl.multiple_of(i * 64, 64), 64), :]
            s = pl.ds(pl.multiple_of(b * 2 * ROWS + i * 64, 64), 64)
            cdf = 0.5 + 0.5 * lax.erf(u * inv)
            acted[k, s, :] = (u * cdf).astype(BF)
            slope = cdf + u * (jnp.exp(-0.5 * u * u) * 0.3989422804014327)
            for c in range(thirds):
                dgelu[k * thirds + c, s, :] = slope[:, c * BQ : (c + 1) * BQ]
            return b

        half(0)
        pl.when(k > 0)(lambda: across(0, k - 1))
        lax.fori_loop(0, 2 * ROWS // 64, act, 0)
        half(1)
        lax.fori_loop(0, 2 * ROWS // 64, act, 1)
        put(0, k, lambda j: mm(acted[k], some(wf, fpart, ff, 2 * ff, j, 2), 1, 1), 2)

    loop(feed)
    across(0, nch - 1)
    fetch.wait()

    def norm_two(k):
        branch = take(0, k) + misc[5:6, :]
        xh, r = moments(first[k] + branch)
        dy = out[rows_of(k), :].astype(F32)
        out[rows_of(k), :] = (xh * misc[1:2, :] + misc[3:4, :]).astype(BF)
        ds = norm_back(dy, misc[1:2, :], xh, r)
        first[k] = ds
        low = ds.astype(BF)
        dff[k, 0] = low
        share(1, k)
        note(2, live(k, branch))
        sums[1:2, :] += col_sum(dy * xh)
        sums[3:4, :] += col_sum(dy)
        sums[5:6, :] += col_sum(low.astype(F32))

    loop(norm_two)

    def feed_back(k):
        shared(1, k)
        def half(b):
            g = dff[k, 2 * b : 2 * b + 2].reshape(2 * ROWS, d)
            for c in range(0, ff, 256):
                pre[:, c : c + 256] = mm(g, whole(wf, fpart, ff + c, ff + c + 256))

        def act(i, b):
            r = pl.ds(pl.multiple_of(i * 64, 64), 64)
            s = pl.ds(pl.multiple_of(b * 2 * ROWS + i * 64, 64), 64)
            slope = jnp.concatenate([dgelu[k * thirds + c, s, :] for c in range(thirds)], axis=1)
            low = (pre[r, :] * slope).astype(BF)
            dpre[k, s, :] = low
            sums[6:7, :] += col_sum(low.astype(F32))
            return b

        half(0)
        pl.when(k > 0)(lambda: across(1, k - 1))
        lax.fori_loop(0, 2 * ROWS // 64, act, 0)
        half(1)
        lax.fori_loop(0, 2 * ROWS // 64, act, 1)
        put(1, k, lambda j: mm(dpre[k], some(wf, fpart, 0, ff, j, 2), 1, 1), 2)

    def weight_part(left, right, to):
        def cols(i, _):
            c = pl.ds(pl.multiple_of(i * 128, 128), 128)
            g = 0.0
            for k in range(nch):
                g = g + mm(left[k, :, :, c].reshape(4 * ROWS, 128), right[k], 0, 0)
            to[c, :] = g.astype(BF)
            return 0

        lax.fori_loop(0, d // 128, cols, 0)

    def norm_one_back(k):
        dy = first[k] + take(1, k)
        xh = xhat[k]
        ds = norm_back(dy, misc[0:1, :], xh, r1[k])
        dfirst[rows_of(k), :] = ds
        low = ds.astype(BF)
        for c in gs[1][:2]:
            c(k).wait_send()
        dff[k, 0] = low
        for j in (3, 2, 1):
            dsend[k, j - 1] = mm(low, wo[j]).astype(BF)
            back(j, k).start()
        dctx[rows_at(t, k), :] = mm(low, wo[0]).astype(BF)
        sums[0:1, :] += col_sum(dy * xh)
        sums[2:3, :] += col_sum(dy)
        sums[4:5, :] += col_sum(low.astype(F32))

    oc = send(ocs, ocr, osem[0].at[0], osem[1].at[0], tensor=core)
    ox = send(oxs, oxr, osem[2].at[0], osem[3].at[0], tensor=cross)

    def out_part():
        x = dff[:, 0].reshape(rows, d)
        for slot, j in ((0, 1), (1, 3)):
            ocs[slot] = mm(x, call[:, j].reshape(rows, width), 0, 0).astype(BF)
        oc.start()

    def out_across():
        p = mm(dff[:, 0].reshape(rows, d), call[:, 2].reshape(rows, width), 0, 0)
        oc.wait_recv()
        oxs[...] = (p + ocr[1].astype(F32)).astype(BF)
        ox.start()

    def out_take():
        p = mm(dff[:, 0].reshape(rows, d), call[:, 0].reshape(rows, width), 0, 0)
        ox.wait_recv()
        gout[...] = (p + ocr[0].astype(F32) + oxr[...].astype(F32)).astype(BF)

    loop(feed_back)
    if ring:
        weight_part(dff, acted, gdown)
        across(1, nch - 1)
        go, close = ring_group(n, place, at, gdown, tracks)
        go()
        norm_one_back(0)
        weight_part(norm, dpre, gup)
        go()
        for k in range(1, nch):
            norm_one_back(k)
            go()
        out_part()
        go()
        out_across()
        go()
        go()
        out_take()
        odown[...] = close()
    else:
        across(1, nch - 1)
        weight_part(dff, acted, gdown)
        weight_part(norm, dpre, gup)
        loop(norm_one_back)
        out_part()
        out_across()
        out_take()

    def finish(k, _):
        end(1, k)
        for j in (1, 2, 3):
            back(j, k).wait_recv()
            back(j, k).wait_send()
            give(j, k).wait_send()
        for c in gs[0] + gs[1][2:]:
            c(k).wait_send()
        return 0

    lax.fori_loop(0, nch, finish, 0)
    for c in slabs + (oc, ox):
        c.wait_send()


def middle(n, qkv, sq, sk, live_row, wg, misc, full, cot, pad, wh, wd, wf):
    ring = wf is None
    vm = pl.BlockSpec(memory_space=pltpu.VMEM)
    rows, d = cot.shape
    width = qkv.shape[2]
    heads = width // DH
    total = 4 * rows
    nch = rows // ROWS
    s = jax.ShapeDtypeStruct
    V = pltpu.VMEM
    ff = wh.shape[1] if ring else wf.shape[2] // 2
    outs = [
        s((rows, d), BF),
        s((rows, d), F32),
        s((total, width), BF),
        s((width, total), F32),
        s((heads, total), F32),
        s((d, width), BF),
        s((d, ff), BF),
        s((d // n, ff), F32) if ring else s((d, ff), BF),
        s((8, d), F32),
    ]
    far = pl.BlockSpec(memory_space=pltpu.HBM)
    pin = lambda x: pltpu.with_memory_space_constraint(x, pltpu.HBM)
    ops = (qkv, sq, sk, live_row, wg, misc, full, pin(cot), pad)
    ops += (pin(wh), pin(wd)) if ring else (wf,)
    g, gr = wg.shape[0], wg.shape[1] - MISC
    wide = -(-width // 128) * 128
    scratch = []
    if ring:
        scratch += [V((n, d // n, 2 * ff), BF), V((d, ff), BF)]
    scratch += [V((total, width), BF), V((nch, 4, ROWS, width), BF), V((3, g, gr, wide), BF), V((4, d, width), BF)]
    scratch += [V((nch, 3, ROWS, width), BF)]
    scratch += [V((nch, 4, ROWS, d), BF)] * 2
    scratch += [V((nch, 4 * ROWS, ff), BF), V((nch * (ff // BQ), 4 * ROWS, BQ), F32), V((2 * ROWS, ff), F32), V((nch, 4 * ROWS, ff), BF)]
    scratch += [V((nch, ROWS, d), F32)] * 2 + [V((nch, ROWS, 1), F32)]
    scratch += [V((nch, 2, ROWS, d), F32), DMA((1,)), DMA((2,))]
    scratch += [V((nch, 2, ROWS, d), BF)] * 2 + [V((nch, ROWS, d), BF)] * 2
    scratch += [V((2, d, width), BF)] * 2 + [V((d, width), BF)] * 2
    scratch += [DMA((2, nch))] * 10 + [DMA((1,))] * 10 + [DMA((nch,))] * 12
    if ring:
        scratch += [DMA((n // 2, 2))] * 4 + ring_scratch(n, d // n, (128,) * (ff // 128))
    return pl.pallas_call(
        functools.partial(middle_kernel, n, ring),
        in_specs=[vm] * 7 + [far, vm] + [far if ring else vm] * (len(ops) - 9),
        out_specs=[vm] * len(outs),
        out_shape=outs,
        scratch_shapes=scratch,
        compiler_params=pltpu.CompilerParams(
            collective_id=2, has_side_effects=True, vmem_limit_bytes=41 << 20
        ),
        name="middle",
    )(*ops)


def last_kernel(n, ring, *refs):
    refs = list(refs)
    pop = lambda m: [refs.pop(0) for _ in range(m)]
    dqkv, wg, full, gout, dfirst, sums = pop(6)
    if ring:
        (gup,) = pop(1)
        dtok, oattn, oout, oup, ogain, oshift, obias, ohb, oqvb, oroot = pop(10)
    else:
        dtok, gb, total = pop(3)
    part, cs, cr, xs, xr = pop(5)
    rsem = pop(4)
    msend, mrecv = pop(2)
    msem = pop(4)
    if ring:
        gb, mall = pop(2)
        mring = pop(4)
        tracks = [refs[i : i + 3] for i in range(0, len(refs), 3)]
    t, f, core, cross, diag, place, at = places(n)
    rows, d = dtok.shape
    nch = rows // ROWS
    wpart = wg.shape[1] - MISC
    w3 = dqkv.shape[1]
    width = w3 // 3
    where = (t, core, cross, diag)
    put, across, take, end = scatter_tools(core, cross, part, cs, cr, xs, xr, rsem)
    nxt, prv = at((place + 1) % n), at((place + n - 1) % n)

    def rows_of(k):
        return pl.ds(pl.multiple_of(k * ROWS, ROWS), ROWS)

    b = col_sum(dqkv[...].astype(F32))
    b = jnp.concatenate([b[:, :width], b[:, 2 * width :], jnp.zeros((1, d - 2 * width), F32)], axis=1)
    msend[0] = sums[...]
    msend[0, 7:8, :] = sums[7:8, :] + b
    meet(core, cross, (nxt, prv) if ring else ())
    m0 = send(msend.at[0], mrecv.at[0], msem[0].at[0], msem[1].at[0], tensor=core)
    m1 = send(msend.at[1], mrecv.at[1], msem[2].at[0], msem[3].at[0], tensor=cross)
    if ring:
        ups = gup.shape[1] // 128
        up, up_close = ring_group(n, place, at, gup, tracks[:ups])
        up()
    m0.start()

    def weight_part(i, _):
        c = pl.ds(pl.multiple_of(i * 128, 128), 128)
        g = 0.0
        for j in range(4):
            g = g + mm(full[j, :, c], dqkv[j * rows : (j + 1) * rows, :], 0, 0)
        gb[c, :] = jnp.concatenate([g.astype(BF), gout[c, :]], axis=1)
        return 0

    lax.fori_loop(0, d // 128, weight_part, 0)
    if ring:
        up()
        own, own_close = ring_group(n, place, at, gb, tracks[ups:])
        own()

        def go():
            up()
            own()

    def tokens_part(k):
        x = jnp.concatenate([dqkv[pl.ds(w * rows + k * ROWS, ROWS), :] for w in where], axis=0)
        put(0, k, lambda j: mm(x, some(wg, wpart, 0, w3, j, 2), 1, 1), 2)

    for k in range(nch):
        tokens_part(k)
        if k > 0:
            across(0, k - 1)
        if ring and k > 0:
            go()
    across(0, nch - 1)
    m0.wait_recv()
    msend[1] = msend[0] + mrecv[0]
    m1.start()
    if ring:
        go()
    m1.wait_recv()
    row = lax.broadcasted_iota(jnp.int32, (8, d), 0)
    col = lax.broadcasted_iota(jnp.int32, (8, d), 1)
    over_tensor = (row < 6) | ((row == 7) & (col >= 2 * width))
    small = jnp.where(over_tensor, msend[1] + mrecv[1], msend[0])

    def keep(k):
        dtok[rows_of(k), :] = dfirst[rows_of(k), :] + take(0, k)

    if ring:
        msend[2] = small
        mall[place] = small
        msteps = []
        far = n // 2
        for s in range(far):
            a, b = (place - s + n) % n, (place + s) % n
            src = msend.at[2] if s == 0 else mall.at[a]
            pair = [send(src, mall.at[a], mring[0].at[s], mring[1].at[s], fsdp=nxt)]
            if s < far - 1:
                src = msend.at[2] if s == 0 else mall.at[b]
                pair.append(send(src, mall.at[b], mring[2].at[s], mring[3].at[s], fsdp=prv))
            msteps.append(pair)
        todo = [functools.partial(keep, k) for k in range(nch)]
        r = 0
        for _ in range(max(nch, far, n)):
            if r < far:
                for i, c in enumerate(msteps[r]):
                    if r > 0:
                        msteps[r - 1][i].wait_recv()
                    c.start()
                r += 1
            go()
            if todo:
                todo.pop(0)()
        msteps[far - 2][1].wait_recv()
        msteps[far - 1][0].wait_recv()
        total = jnp.sum(mall[...], axis=0)
        gp = d // n
        mine = pltpu.roll(total, (d - f * gp) % d, 1)
        ogain[...] = mine[0:2, :gp]
        oshift[...] = mine[2:4, :gp]
        obias[...] = mine[4:6, :gp]
        k = DH // n
        mine = pltpu.roll(total, (d - f * k) % d, 1)
        ohb[...] = jnp.concatenate([mine[6:7, h * DH : (h + 1) * DH] for h in range(ohb.shape[1])], axis=0).T[:k]
        heads = oqvb.shape[0]
        for h in range(heads):
            for j in range(2):
                c = (j * heads + h) * DH
                oqvb[h, j : j + 1, :] = mine[7:8, c : c + DH][:, :k]
        spot = lax.broadcasted_iota(jnp.int32, (1, d), 1) - d // 2
        pick = lambda j: jnp.sum(jnp.where(spot == j, total[7:8], 0.0), axis=1, keepdims=True)
        count = pick(3)
        col = lax.broadcasted_iota(jnp.int32, (1, 128), 1)
        o = jnp.zeros((1, 128), F32)
        for j in range(3):
            o = jnp.where(col == j, jnp.sqrt(pick(j) / (count * d)), o)
        oroot[...] = o
        oup[...] = up_close()
        x = own_close()
        for j in range(3):
            oattn[j] = x[:, j * width : (j + 1) * width]
        oout[...] = x[:, 3 * width :].T
        for pair in msteps:
            for c in pair:
                c.wait_send()
    else:
        total[...] = small
        for k in range(nch):
            keep(k)

    def finish(k, _):
        end(0, k)
        return 0

    lax.fori_loop(0, nch, finish, 0)
    m0.wait_send()
    m1.wait_send()


def last(n, ring, dqkv, wg, full, gout, dfirst, sums, gup):
    vm = pl.BlockSpec(memory_space=pltpu.VMEM)
    rows, d = dfirst.shape
    width = dqkv.shape[1] // 3
    heads = width // DH
    nch = rows // ROWS
    s = jax.ShapeDtypeStruct
    V = pltpu.VMEM
    ops = (dqkv, wg, full, gout, dfirst, sums)
    outs = [s((rows, d), F32)]
    gp = d // n
    k = DH // n
    if ring:
        ops += (gup,)
        outs += [s((3, gp, width), F32), s((width, gp), F32), s((gp, gup.shape[1]), F32)] + [s((2, gp), F32)] * 3
        outs += [s((k, d // DH), F32), s((heads, 2, k), F32), s((1, 128), F32)]
    else:
        outs += [s((d, d), BF), s((8, d), F32)]
    scratch = [V((nch, 2, ROWS, d), F32)]
    scratch += [V((nch, 2, ROWS, d), BF)] * 2 + [V((nch, ROWS, d), BF)] * 2
    scratch += [DMA((1, nch))] * 4
    scratch += [V((3, 8, d), F32), V((2, 8, d), F32)] + [DMA((1,))] * 4
    if ring:
        scratch += [V((d, d), BF), V((n, 8, d), F32)] + [DMA((n // 2,))] * 4
        scratch += ring_scratch(n, gp, (128,) * ((gup.shape[1] + d) // 128))
    return pl.pallas_call(
        functools.partial(last_kernel, n, ring),
        in_specs=[vm] * len(ops),
        out_specs=[vm] * len(outs),
        out_shape=outs,
        scratch_shapes=scratch,
        compiler_params=pltpu.CompilerParams(
            collective_id=3, has_side_effects=True, vmem_limit_bytes=12 << 20
        ),
        name="last",
    )(*ops)


def deliver_kernel(*refs):
    m = (len(refs) - 3) // 2
    src, roots, dst, three, sem = refs[:m], refs[m], refs[m + 1 : -2], refs[-2], refs[-1]
    for j in range(m):
        pltpu.make_async_copy(src[j], dst[j], sem.at[j]).start()
    for j in range(three.shape[0]):
        three[j] = jnp.sum(roots[0:1, j : j + 1])
    for j in range(m):
        pltpu.make_async_copy(src[j], dst[j], sem.at[j]).wait()


def deliver(arrays, roots):
    vm = pl.BlockSpec(memory_space=pltpu.VMEM)
    return pl.pallas_call(
        deliver_kernel,
        in_specs=[vm] * (len(arrays) + 1),
        out_specs=[pl.BlockSpec(memory_space=pl.ANY)] * len(arrays) + [pl.BlockSpec(memory_space=pltpu.SMEM)],
        out_shape=[jax.ShapeDtypeStruct(x.shape, x.dtype) for x in arrays] + [jax.ShapeDtypeStruct((3,), F32)],
        scratch_shapes=[DMA((len(arrays),))],
        compiler_params=pltpu.CompilerParams(vmem_limit_bytes=1 << 20),
        name="deliver",
    )(*arrays, roots)


def bwd_kernel(heads, bounds, qkv_ref,dc_ref,oct_ref,lse_ref,sq_ref,sk_ref,pad_ref, dqkv_ref, qt, dt, kt, kh, vh, qh, dh, dqt, dsum, dka, dva):
    S=qkv_ref.shape[1]; W=heads*DH
    qs=(qkv_ref[0].astype(F32)*0.125)
    qsb=qs.astype(BF); qt[...]=qs.T.astype(BF)
    kk=qkv_ref[1]; vv=qkv_ref[2]
    kt[...]=kk.astype(F32).T.astype(BF)
    dct=dc_ref[...].astype(F32).T*pad_ref[0:1,:]
    dt[...]=dct.astype(BF)
    dcn=dct.T.astype(BF)
    prod=dct*oct_ref[...]
    for h in range(heads):
        c=slice(h*DH,(h+1)*DH)
        kh[h]=kk[:,c]; vh[h]=vv[:,c]; qh[h]=qsb[:,c]; dh[h]=dcn[:,c]
        dsum[h:h+1,:]=jnp.sum(prod[h*DH:(h+1)*DH],axis=0,keepdims=True)
    dqt[...]=jnp.zeros_like(dqt)
    def kblock(j,_):
        k0=pl.multiple_of(j*BK,BK)
        lo=bounds[2*j]; hi=bounds[2*j+1]
        sk=jnp.concatenate([sk_ref[pl.ds(k0,BK),:]]*(BQ//128),axis=1)
        kpos=k0+lax.broadcasted_iota(jnp.int32,(BK,BQ),0)
        dka[...]=jnp.zeros_like(dka); dva[...]=jnp.zeros_like(dva)
        def body(i,_):
            q0=pl.multiple_of(i*BQ,BQ)
            sq=sq_ref[0:1,pl.ds(q0,BQ)]
            qpos=q0+lax.broadcasted_iota(jnp.int32,(BK,BQ),1)
            ok=(sk==sq)|(kpos==qpos)
            for h in range(heads):
                r=slice(h*DH,(h+1)*DH)
                s=jnp.where(ok,mm(kh[h,pl.ds(k0,BK),:],qt[r,pl.ds(q0,BQ)]),-1e30)
                p=jnp.exp(s-lse_ref[h:h+1,pl.ds(q0,BQ)])
                dp=mm(vh[h,pl.ds(k0,BK),:],dt[r,pl.ds(q0,BQ)])
                ds=(p*(dp-dsum[h:h+1,pl.ds(q0,BQ)])).astype(BF)
                dva[h]+=mm(p.astype(BF),dh[h,pl.ds(q0,BQ),:])
                dka[h]+=mm(ds,qh[h,pl.ds(q0,BQ),:])
                dqt[r,pl.ds(q0,BQ)]+=mm(kt[r,pl.ds(k0,BK)],ds)
            return 0
        lax.fori_loop(lo,hi,body,0)
        dqkv_ref[pl.ds(k0,BK),W:]=jnp.concatenate([dka[h] for h in range(heads)]+[dva[h] for h in range(heads)],axis=1).astype(BF)
        return 0
    lax.fori_loop(0,S//BK,kblock,0)
    dqkv_ref[:,:W]=(dqt[...]*0.125).T.astype(BF)

def attn_bwd(bounds,qkv,dc,oct,lse,sq,sk,pad):
    _,S,W=qkv.shape; heads=W//DH
    vm=pl.BlockSpec(memory_space=pltpu.VMEM)
    return pl.pallas_call(functools.partial(bwd_kernel,heads),
        in_specs=[pl.BlockSpec(memory_space=pltpu.SMEM)]+[vm]*7,
        out_specs=vm,
        out_shape=jax.ShapeDtypeStruct((S,3*W),BF),
        scratch_shapes=[pltpu.VMEM((W,S),BF)]*3+[pltpu.VMEM((heads,S,DH),BF)]*4+[pltpu.VMEM((W,S),F32),pltpu.VMEM((heads,S),F32)]+[pltpu.VMEM((heads,BK,DH),F32)]*2,
        compiler_params=pltpu.CompilerParams(vmem_limit_bytes=13<<20),
        name="attend_backward")(bounds,qkv,dc,oct,lse,sq,sk,pad)


def split_up(value, dim, devices):
    before, after = (value.shape[:dim], value.shape[dim + 1 :])
    return jnp.moveaxis(value.reshape(*before, devices, -1, *after), dim, 0)


def summed_on_arrival(value, axis, dim):
    blocks = split_up(value, dim, lax.axis_size(axis))
    arrived = lax.all_to_all(blocks, axis, split_axis=0, concat_axis=0, tiled=True)
    return arrived.astype(F32).sum(axis=0)


def shards(
    tokens,
    attn_weight,
    query_value_bias,
    out_weight,
    hidden_weight,
    hidden_bias,
    down_weight,
    norm_gains,
    norm_biases,
    output_biases,
    segment_ids,
    padding,
    cotangent,
):
    n = lax.axis_size("fsdp")
    f = lax.axis_index("fsdp")
    t = lax.axis_index("tensor")
    rows, d = tokens.shape
    gp = d // n
    width = attn_weight.shape[2]
    heads = width // DH
    ff = hidden_weight.shape[1]
    ring = gp % 16 == 0 and n % 2 == 0 and n >= 4
    if ring:
        raw = (
            attn_weight,
            out_weight,
            norm_gains,
            norm_biases,
            output_biases,
            hidden_bias.T,
            query_value_bias.transpose(1, 0, 2),
        )
        got = project(n, tokens, width, segment_ids, padding, raw=raw)
        wh, wd, wf = hidden_weight, down_weight.T, None
    else:
        gather = lambda x, dim: lax.all_gather(x, "fsdp", axis=dim, tiled=True)
        w = gather(attn_weight, 1).transpose(1, 0, 2).reshape(d, 3 * width)
        wo = gather(out_weight, 1).T
        b = gather(query_value_bias, 2).reshape(2, width)
        b = jnp.concatenate([b[0], jnp.zeros((width,), BF), b[1], jnp.zeros((width,), BF)])
        misc = jnp.concatenate(
            [
                gather(norm_gains, 1),
                gather(norm_biases, 1),
                gather(output_biases, 1),
                gather(hidden_bias, 1).reshape(1, ff),
                b[None],
                jnp.zeros((MISC - 8, d), BF),
            ]
        )
        wg = jnp.concatenate([jnp.concatenate([w, wo], axis=1), misc])[None]
        got = project(n, tokens, width, segment_ids, padding, wg=wg)
        wf = jnp.concatenate([gather(hidden_weight, 0), gather(down_weight, 1).T], axis=1)[None]
        wh = wd = None
    full, qkv, misc, seg_row, seg_keys, pad_row, pad_cols, bounds, wg = got
    layer_out, d_first, d_ctx, ctx_t, lse, g_out, g_hidden, g_down, sums = middle(
        n, qkv, seg_row, seg_keys, pad_row, wg, misc, full, cotangent, pad_cols, wh, wd, wf
    )
    d_qkv = attn_bwd(bounds, qkv, d_ctx, ctx_t, lse, seg_row, seg_keys, pad_row)
    done = last(n, ring, d_qkv, wg, full, g_out, d_first, sums, g_hidden)
    if ring:
        done = deliver((layer_out, g_down) + tuple(done[:-1]), done[-1])
        layer_out, g_down, d_tokens, g_attn, g_proj, g_hidden, g_gain, g_shift, g_bias, g_hb, g_qvb, roots = done
        g_down = g_down.T
        g_hb = g_hb.T
        g_qvb = g_qvb.transpose(1, 0, 2)
    else:
        d_tokens, g, total = done
        total = lax.psum(total, "fsdp")
        g_attn = g[:, : 3 * width].reshape(d, 3, width).transpose(1, 0, 2)
        g_attn = summed_on_arrival(g_attn, "fsdp", 1)
        g_proj = summed_on_arrival(g[:, 3 * width :].T, "fsdp", 1)
        g_hidden = summed_on_arrival(g_hidden, "fsdp", 0)
        g_down = summed_on_arrival(g_down.T, "fsdp", 1)
        vectors = lax.dynamic_slice(total, (0, f * gp), (6, gp))
        g_gain, g_shift, g_bias = vectors[0:2], vectors[2:4], vectors[4:6]
        k = DH // n
        g_hb = lax.dynamic_slice(total[6].reshape(ff // DH, DH), (0, f * k), (ff // DH, k))
        g_qvb = lax.dynamic_slice(
            total[7, : 2 * width].reshape(2 * heads, DH), (0, f * k), (2 * heads, k)
        ).reshape(2, heads, k)
        squares = total[7, d // 2 : d // 2 + 4]
        roots = jnp.sqrt(squares[:3] / (squares[3] * d))
    return (
        layer_out,
        d_tokens,
        g_attn,
        g_qvb,
        g_proj,
        g_hidden,
        g_hb,
        g_down,
        g_gain,
        g_shift,
        g_bias,
        roots,
    )


def solution(mesh):
    placed = (
        P(("fsdp", "tensor"), None),
        P(None, "fsdp", "tensor"),
        P(None, "tensor", "fsdp"),
        P("tensor", "fsdp"),
        P("fsdp", "tensor"),
        P("tensor", "fsdp"),
        P("tensor", "fsdp"),
        P(None, "fsdp"),
        P(None, "fsdp"),
        P(None, "fsdp"),
        P("fsdp"),
        P("fsdp"),
        P(("fsdp", "tensor"), None),
    )
    return jax.shard_map(
        shards,
        mesh=mesh,
        in_specs=placed,
        out_specs=(
            P(("fsdp", "tensor"), None),
            P(("fsdp", "tensor"), None),
            P(None, "fsdp", "tensor"),
            P(None, "tensor", "fsdp"),
            P("tensor", "fsdp"),
            P("fsdp", "tensor"),
            P("tensor", "fsdp"),
            P("tensor", "fsdp"),
            P(None, "fsdp"),
            P(None, "fsdp"),
            P(None, "fsdp"),
            P(),
        ),
        check_vma=False,
    )
```

profile of v0, /device:TPU:0, one launch (start us, length us, event | category | flops | bytes accessed | tf_op | source)
XLA Modules:
  0.0 197.0 jit_solution(15799956995797339108)
XLA Ops:
  0.6 28.3 %project.1 = (bf16[4,384,768]{2,1,0:T(8,128)(2,1)S(1)}, bf16[3,1536,192]{2,1,0:T(8,128)(2,1)S(1)}, f32[16,768]{1,0:T(8,128)S(1)}, f32[1,1536]{1,0:T(1,128)S(1)},...) custom-call(bf16[384,768]{1,0:T(8,128)(2,1)} %refs_0_.1, ...), custom_call_target="tpu_custom_call" | custom-call | tf_op jit(solution)/shard_map/project/pallas_call | solution.py:266
  28.9 102.9 %middle.1 = (bf16[384,768]{1,0:T(8,128)(2,1)S(1)}, f32[384,768]{1,0:T(8,128)S(1)}, bf16[1536,192]{1,0:T(8,128)(2,1)S(1)}, f32[192,1536]{1,0:T(8,128)S(1)}, f32[3...) custom-call(bf16[3,1536,192]{2,1,0:T(8,128)(2,1)S(1)} %get-tuple-ele, ...), custom_call_target="tpu_custom_call" | custom-call | tf_op jit(solution)/shard_map/middle/pallas_call | solution.py:866
  131.8 21.3 %attend_backward.1.refs_0_ = bf16[1536,576]{1,0:T(8,128)(2,1)S(1)} custom-call(s32[12]{0:T(128)S(1)} %get-tuple-element.62.bounds, bf16[3,1536,192]{2,1,0:T(8,128)(2,1)S(1)} %get-tuple-element.52.refs_0_.qkv_ref, bf16[1536,192]{1,0:T(8,128)(2,1)S(1)} %get-tuple-element.63.dc_ref, f32[192,1536]{1,0:T(8,128)S(1)} %get-tuple-element.64.oct_ref, ...), custom_call_target="tpu_custom_call" | custom-call | tf_op jit(solution)/shard_map/attend_backward/pallas_call | solution.py:1143
  153.1 41.6 %last.1 = (f32[384,768]{1,0:T(8,128)S(1)}, f32[3,96,192]{2,1,0:T(8,128)S(1)}, f32[192,96]{1,0:T(8,128)S(1)}, f32[96,768]{1,0:T(8,128)S(1)}, f32[2,96]{1,0:T(2,12...) custom-call(bf16[1536,576]{1,0:T(8,128)(2,1)S(1)} %attend_backward.1, ...), custom_call_target="tpu_custom_call" | custom-call | tf_op jit(solution)/shard_map/last/pallas_call | solution.py:1061
  194.7 2.2 %deliver.1 = (bf16[384,768]{1,0:T(8,128)(2,1)}, f32[96,768]{1,0:T(8,128)}, f32[384,768]{1,0:T(8,128)}, f32[3,96,192]{2,1,0:T(8,128)}, f32[192,96]{1,0:T(8,128)},...) custom-call(bf16[384,768]{1,0:T(8,128)(2,1)S(1)} %get-tuple-element., ...), custom_call_target="tpu_custom_call" | custom-call | tf_op jit(solution)/shard_map/deliver/pallas_call | solution.py:1087
where the time goes:
time: 197 us
  Pallas kernels  196 us (99%)
    pallas_call x1, Pallas kernels, middle(): pl.pallas_call(functools.partial(middle_kernel, n, ring), in_specs=[vm] *...  103 us
    pallas_call x1, Pallas kernels, last(): pl.pallas_call(functools.partial(last_kernel, n, ring), in_specs=[vm] * l...  41.6 us
    pallas_call x1, Pallas kernels, project(): pl.pallas_call(functools.partial(project_kernel, n, ring), in_specs=[pl.B...  28.3 us
    pallas_call x1, Pallas kernels, attn_bwd(): pl.pallas_call(functools.partial(bwd_kernel, heads), in_specs=[pl.BlockSp...  21.3 us

commit v1 on v0

--- a/solution.py
+++ b/solution.py
@@ -123,23 +123,14 @@
     return jnp.sum(fold_sum(s), axis=0, keepdims=True)
 
 
-def project_kernel(n, ring, *refs):
-    refs = list(refs)
-    pop = lambda m: [refs.pop(0) for _ in range(m)]
-    tok, seg, alive = pop(3)
-    if ring:
-        far = [seg, alive] + pop(7)
-    else:
-        (wg,) = pop(1)
-    full, qkv, misc, sq, sk, live, lives, bounds = pop(8)
-    if ring:
-        wg, mine = pop(2)
-        near = pop(len(far))
-        nsem = pop(1)[0]
+def project_part(n, ring, tok, far, outs, wg, mine, near, nsem, sems, gsems, lead, follow, ready):
+    full, qkv, misc, sq, sk, live, lives, bounds = outs
+    if ring:
         for j in range(len(far)):
             pltpu.make_async_copy(far[j], near[j], nsem.at[j]).start()
-    lsem, xs, xr, cs, cr, fs, fr = pop(7)
-    gsems = refs
+    else:
+        seg, alive = far
+    lsem, xs, xr, cs, cr, fs, fr = sems
     t, f, core, cross, diag, place, at = places(n)
     rows, d = tok.shape
     part = wg.shape[1] - MISC
@@ -169,9 +160,10 @@
             b = jnp.where(col == j, x[0:1], jnp.where(col == 2 * heads + j, x[1:2], b))
         mine[part:] = jnp.concatenate(wide + [h, b, jnp.zeros((8, d), F32)], axis=0).astype(BF)
         steps = both_ways(n, place, at, mine, wg, gsems)
-        meet(core, cross, (at((place + 1) % n), at((place + n - 1) % n)))
+        lead()
+        meet(core, cross, (at((place + 1) % n), at((place + n - 1) % n)), diag)
     else:
-        meet(core, cross, ())
+        meet(core, cross, (), diag)
     R = range(rows // ROWS)
     cut = lambda i: pl.ds(i * ROWS, ROWS)
     xc = [send(tok.at[cut(i)], full.at[t, cut(i)], xs.at[i], xr.at[i], tensor=cross) for i in R]
@@ -206,6 +198,7 @@
     if ring:
         for s in range(1, len(steps)):
             ring_on(steps, s)
+        follow()
     for i in R:
         xc[i].wait_recv()
         fc[i].start()
@@ -215,6 +208,7 @@
         c.wait_recv()
     if ring:
         ring_end(steps)
+    ready()
     misc[...] = jnp.sum(wg[:, part:, :].astype(F32), axis=0)
     w = 3 * head
 
@@ -233,48 +227,6 @@
     block(diag)
     for c in xc + cc + fc:
         c.wait_send()
-
-
-def project(n, tok, head, seg, alive, raw=None, wg=None):
-    ring = wg is None
-    vm = pl.BlockSpec(memory_space=pltpu.VMEM)
-    rows, d = tok.shape
-    nch = rows // ROWS
-    s = jax.ShapeDtypeStruct
-    total = 4 * rows
-    outs = [
-        s((4, rows, d), BF),
-        s((3, total, head), BF),
-        s((MISC, d), F32),
-        s((1, total), F32),
-        s((total, 128), F32),
-        s((1, total), F32),
-        s((total, 128), F32),
-        s((2 * total // BQ,), jnp.int32),
-    ]
-    specs = [vm] * 7 + [pl.BlockSpec(memory_space=pltpu.SMEM)]
-    scratch = [DMA((2,))] + [DMA((nch,))] * 6
-    ops = (tok, seg.reshape(-1, 128), alive.reshape(-1, 128))
-    if ring:
-        ops = tuple(pltpu.with_memory_space_constraint(x, pltpu.HBM) for x in ops + raw)
-        outs.append(s((n, d // n + MISC, d), BF))
-        specs.append(vm)
-        held = [pltpu.VMEM(x.shape, x.dtype) for x in ops[1:]]
-        scratch = [pltpu.VMEM((d // n + MISC, d), BF)] + held + [DMA((len(held),))] + scratch + [DMA((n // 2, 2))] * 4
-    else:
-        ops += (wg,)
-    got = pl.pallas_call(
-        functools.partial(project_kernel, n, ring),
-        in_specs=[pl.BlockSpec(memory_space=pltpu.HBM) if ring else vm] * len(ops),
-        out_specs=specs,
-        out_shape=outs,
-        scratch_shapes=scratch,
-        compiler_params=pltpu.CompilerParams(
-            collective_id=1, has_side_effects=True, vmem_limit_bytes=2 << 20
-        ),
-        name="project",
-    )(*ops)
-    return tuple(got) if ring else tuple(got) + (wg,)
 
 
 def moments(h):
@@ -337,45 +289,57 @@
 
 
 class RingSum:
-    def __init__(self, n, place, at, local, c0, c1, rbuf, ss, rs, right):
-        self.n, self.rbuf = n, rbuf
-        target = at((place + 1) % n) if right else at((place + n - 1) % n)
-        step = -1 if right else 1
-        self.own = lambda s: block_rows(local, at((place + step * (1 + s) + 2 * n) % n), c0, c1, n)
-
-        def copy(s):
-            src = self.own(0) if s == 0 else rbuf.at[s - 1]
-            return send(src, rbuf.at[s], ss.at[s], rs.at[s], fsdp=target)
-
-        self.copy = copy
+    def __init__(self, n, place, at, local, c0, c1, buf, ss, rs, longer):
+        nxt, prv = at((place + 1) % n), at((place + n - 1) % n)
+        right = n // 2 if longer else n - 1 - n // 2
+        self.buf, self.local = buf, lambda p: block_rows(local, at((p + n) % n), c0, c1, n)
+        self.place = place
+        self.chains = (
+            (0, right, lambda s: place + right - s, nxt),
+            (right, n - 1 - right, lambda s: place - (n - 1 - right) + s, prv),
+        )
+        self.ss, self.rs = ss, rs
+
+    def copy(self, chain, s):
+        base, _, owner, target = chain
+        src = self.local(owner(0)) if s == 0 else self.buf.at[base + s - 1]
+        j = base + s
+        return send(src, self.buf.at[j], self.ss.at[j], self.rs.at[j], fsdp=target)
 
     def go(self, s):
-        if s > 0:
-            self.copy(s - 1).wait_recv()
-            self.rbuf[s - 1] = (self.rbuf[s - 1].astype(F32) + self.own(s)[...].astype(F32)).astype(BF)
-        self.copy(s).start()
+        for chain in self.chains:
+            base, hops, owner, _ = chain
+            if s >= hops:
+                continue
+            if s > 0:
+                self.copy(chain, s - 1).wait_recv()
+                j = base + s - 1
+                self.buf[j] = (self.buf[j].astype(F32) + self.local(owner(s))[...].astype(F32)).astype(BF)
+            self.copy(chain, s).start()
 
     def close(self):
-        s = self.n - 2
-        self.copy(s).wait_recv()
-        return self.rbuf[s].astype(F32) + self.own(s + 1)[...].astype(F32)
+        total = self.local(self.place)[...].astype(F32)
+        for chain in self.chains:
+            self.copy(chain, chain[1] - 1).wait_recv()
+            total = total + self.buf[chain[0] + chain[1] - 1].astype(F32)
+        return total
 
     def sent(self):
-        for s in range(self.n - 1):
-            self.copy(s).wait_send()
+        for chain in self.chains:
+            for s in range(chain[1]):
+                self.copy(chain, s).wait_send()
 
 
 def ring_group(n, place, at, local, tracks):
     m = len(tracks)
-    q = [RingSum(n, place, at, local, j * 128, j * 128 + 128, *tracks[j], j < m // 2) for j in range(m)]
-    left = list(range(n - 1))
+    q = [RingSum(n, place, at, local, j * 128, j * 128 + 128, *tracks[j], j % 2) for j in range(m)]
+    left = list(range(n // 2))
 
     def go():
         if left:
             s = left.pop(0)
-            for j in range(m // 2):
-                q[j].go(s)
-                q[j + m // 2].go(s)
+            for r in q:
+                r.go(s)
 
     def close():
         while left:
@@ -441,22 +405,35 @@
 def middle_kernel(n, ring, *refs):
     refs = list(refs)
     pop = lambda m: [refs.pop(0) for _ in range(m)]
-    qkv, sq, sk, live_row, wg, misc, full, cot_hbm, pad = pop(9)
+    tok, cot_hbm = pop(2)
+    raw = pop(9 if ring else 2)
     if ring:
         wh, wd = pop(2)
     else:
-        (wf,) = pop(1)
-    out, dfirst, dctx, octx, lse, gout, gup, odown, sums = pop(9)
+        wg, wf = pop(2)
+    full, qkv, sq, sk, live_row, bounds = pop(6)
+    if ring:
+        (wg,) = pop(1)
+    out, dfirst, dctx, octx, lse, gown, gsend, gup, odown, sums = pop(10)
     gdown = odown
+    misc, pad = pop(2)
+    mine = near = nsem = psems = None
+    if ring:
+        mine = pop(1)[0]
+        near = pop(len(raw))
+        nsem = pop(1)[0]
+    tsems = pop(7)
+    if ring:
+        psems = pop(4)
     if ring:
         (wf, gdown) = pop(2)
     ctx, call, slab, wo, dsend = pop(5)
     (norm, dff, acted, dgelu, pre, dpre, first, xhat, r1, part, csem, lsem) = pop(12)
     cs, cr, xs, xr = pop(4)
-    ocs, ocr, oxs, oxr = pop(4)
+    ocs, ocr = pop(2)
     rsem = pop(4)
     gsem = pop(6)
-    osem = pop(4)
+    osem = pop(2)
     ssem = pop(6)
     asem = pop(6)
     dsem = pop(6)
@@ -494,10 +471,10 @@
         gs[i][2](k).wait_recv()
 
     lane0 = d - slab.shape[-1]
-    mine = wg.at[:, pl.ds(0, wpart), pl.ds(lane0, slab.shape[-1])]
+    slab0 = wg.at[:, pl.ds(0, wpart), pl.ds(lane0, slab.shape[-1])]
     slabs = (
-        send(mine, slab.at[1], ssem[0].at[0], ssem[1].at[0], tensor=cross),
-        send(mine, slab.at[0], ssem[2].at[0], ssem[3].at[0], tensor=core),
+        send(slab0, slab.at[1], ssem[0].at[0], ssem[1].at[0], tensor=cross),
+        send(slab0, slab.at[0], ssem[2].at[0], ssem[3].at[0], tensor=core),
         send(slab.at[1], slab.at[2], ssem[4].at[0], ssem[5].at[0], tensor=core),
     )
 
@@ -510,23 +487,31 @@
     def back(j, k):
         return send(dsend.at[k, j - 1], dctx.at[rows_at(t, k), :], dsem[2 * j - 2].at[k], dsem[2 * j - 1].at[k], tensor=where[j])
 
+    load = []
+    steps = []
     if ring:
         load = [
             pltpu.make_async_copy(wh, wf.at[f, :, pl.ds(0, ff)], lsem.at[0]),
             pltpu.make_async_copy(wd, wf.at[f, :, pl.ds(ff, ff)], lsem.at[1]),
         ]
+        steps = both_ways(n, place, at, wf.at[f], wf, wsem)
+
+    def lead():
         for c in load:
             c.start()
+
+    def follow():
         for c in load:
             c.wait()
-        steps = both_ways(n, place, at, wf.at[f], wf, wsem)
-        meet(core, cross, (at((place + 1) % n), at((place + n - 1) % n)), diag)
         for c in steps[0]:
             c.start()
-    else:
-        meet(core, cross, (), diag)
-    slabs[0].start()
-    slabs[1].start()
+
+    def ready():
+        slabs[0].start()
+        slabs[1].start()
+
+    outs = (full, qkv, misc, sq, sk, live_row, pad, bounds)
+    project_part(n, ring, tok, raw, outs, wg, mine, near, nsem, tsems, psems, lead, follow, ready)
     sums[...] = jnp.zeros_like(sums)
 
     blocks = 4 * rows // BQ
@@ -759,7 +744,6 @@
         sums[4:5, :] += col_sum(low.astype(F32))
 
     oc = send(ocs, ocr, osem[0].at[0], osem[1].at[0], tensor=core)
-    ox = send(oxs, oxr, osem[2].at[0], osem[3].at[0], tensor=cross)
 
     def out_part():
         x = dff[:, 0].reshape(rows, d)
@@ -767,16 +751,13 @@
             ocs[slot] = mm(x, call[:, j].reshape(rows, width), 0, 0).astype(BF)
         oc.start()
 
-    def out_across():
-        p = mm(dff[:, 0].reshape(rows, d), call[:, 2].reshape(rows, width), 0, 0)
-        oc.wait_recv()
-        oxs[...] = (p + ocr[1].astype(F32)).astype(BF)
-        ox.start()
-
     def out_take():
-        p = mm(dff[:, 0].reshape(rows, d), call[:, 0].reshape(rows, width), 0, 0)
-        ox.wait_recv()
-        gout[...] = (p + ocr[0].astype(F32) + oxr[...].astype(F32)).astype(BF)
+        x = dff[:, 0].reshape(rows, d)
+        for slot, j, to in ((1, 2, gsend), (0, 0, gown)):
+            p = mm(x, call[:, j].reshape(rows, width), 0, 0)
+            if slot:
+                oc.wait_recv()
+            to[...] = (p + ocr[slot].astype(F32)).astype(BF)
 
     loop(feed_back)
     if ring:
@@ -792,9 +773,6 @@
             go()
         out_part()
         go()
-        out_across()
-        go()
-        go()
         out_take()
         odown[...] = close()
     else:
@@ -803,7 +781,6 @@
         weight_part(norm, dpre, gup)
         loop(norm_one_back)
         out_part()
-        out_across()
         out_take()
 
     def finish(k, _):
@@ -817,40 +794,63 @@
         return 0
 
     lax.fori_loop(0, nch, finish, 0)
-    for c in slabs + (oc, ox):
+    for c in slabs + (oc,):
         c.wait_send()
 
 
-def middle(n, qkv, sq, sk, live_row, wg, misc, full, cot, pad, wh, wd, wf):
+def middle(n, tok, cot, head, seg, alive, raw, wh, wd, wg, wf):
     ring = wf is None
     vm = pl.BlockSpec(memory_space=pltpu.VMEM)
+    far = pl.BlockSpec(memory_space=pltpu.HBM)
+    pin = lambda x: pltpu.with_memory_space_constraint(x, pltpu.HBM)
     rows, d = cot.shape
-    width = qkv.shape[2]
+    width = head
     heads = width // DH
     total = 4 * rows
     nch = rows // ROWS
     s = jax.ShapeDtypeStruct
     V = pltpu.VMEM
     ff = wh.shape[1] if ring else wf.shape[2] // 2
+    tables = (seg.reshape(-1, 128), alive.reshape(-1, 128))
+    if ring:
+        ops = tuple(pin(x) for x in (tok, cot) + tables + raw + (wh, wd))
+        specs = [far] * len(ops)
+    else:
+        ops = (tok, pin(cot)) + tables + (wg, wf)
+        specs = [vm, far] + [vm] * 4
     outs = [
+        s((4, rows, d), BF),
+        s((3, total, width), BF),
+        s((1, total), F32),
+        s((total, 128), F32),
+        s((1, total), F32),
+        s((2 * total // BQ,), jnp.int32),
+    ]
+    ospecs = [vm] * 5 + [pl.BlockSpec(memory_space=pltpu.SMEM)]
+    if ring:
+        outs.append(s((n, d // n + MISC, d), BF))
+    outs += [
         s((rows, d), BF),
         s((rows, d), F32),
         s((total, width), BF),
         s((width, total), F32),
         s((heads, total), F32),
         s((d, width), BF),
+        s((d, width), BF),
         s((d, ff), BF),
         s((d // n, ff), F32) if ring else s((d, ff), BF),
         s((8, d), F32),
     ]
-    far = pl.BlockSpec(memory_space=pltpu.HBM)
-    pin = lambda x: pltpu.with_memory_space_constraint(x, pltpu.HBM)
-    ops = (qkv, sq, sk, live_row, wg, misc, full, pin(cot), pad)
-    ops += (pin(wh), pin(wd)) if ring else (wf,)
-    g, gr = wg.shape[0], wg.shape[1] - MISC
+    ospecs += [vm] * (len(outs) - len(ospecs))
+    g, gr = (n, d // n) if ring else (wg.shape[0], wg.shape[1] - MISC)
     wide = -(-width // 128) * 128
-    scratch = []
-    if ring:
+    scratch = [V((MISC, d), F32), V((total, 128), F32)]
+    if ring:
+        held = tables + raw
+        scratch += [V((d // n + MISC, d), BF)] + [V(x.shape, x.dtype) for x in held] + [DMA((len(held),))]
+    scratch += [DMA((2,))] + [DMA((nch,))] * 6
+    if ring:
+        scratch += [DMA((n // 2, 2))] * 4
         scratch += [V((n, d // n, 2 * ff), BF), V((d, ff), BF)]
     scratch += [V((total, width), BF), V((nch, 4, ROWS, width), BF), V((3, g, gr, wide), BF), V((4, d, width), BF)]
     scratch += [V((nch, 3, ROWS, width), BF)]
@@ -859,18 +859,18 @@
     scratch += [V((nch, ROWS, d), F32)] * 2 + [V((nch, ROWS, 1), F32)]
     scratch += [V((nch, 2, ROWS, d), F32), DMA((1,)), DMA((2,))]
     scratch += [V((nch, 2, ROWS, d), BF)] * 2 + [V((nch, ROWS, d), BF)] * 2
-    scratch += [V((2, d, width), BF)] * 2 + [V((d, width), BF)] * 2
-    scratch += [DMA((2, nch))] * 10 + [DMA((1,))] * 10 + [DMA((nch,))] * 12
+    scratch += [V((2, d, width), BF)] * 2
+    scratch += [DMA((2, nch))] * 10 + [DMA((1,))] * 8 + [DMA((nch,))] * 12
     if ring:
         scratch += [DMA((n // 2, 2))] * 4 + ring_scratch(n, d // n, (128,) * (ff // 128))
     return pl.pallas_call(
         functools.partial(middle_kernel, n, ring),
-        in_specs=[vm] * 7 + [far, vm] + [far if ring else vm] * (len(ops) - 9),
-        out_specs=[vm] * len(outs),
+        in_specs=specs,
+        out_specs=ospecs,
         out_shape=outs,
         scratch_shapes=scratch,
         compiler_params=pltpu.CompilerParams(
-            collective_id=2, has_side_effects=True, vmem_limit_bytes=41 << 20
+            collective_id=2, has_side_effects=True, vmem_limit_bytes=38 << 20
         ),
         name="middle",
     )(*ops)
@@ -879,7 +879,7 @@
 def last_kernel(n, ring, *refs):
     refs = list(refs)
     pop = lambda m: [refs.pop(0) for _ in range(m)]
-    dqkv, wg, full, gout, dfirst, sums = pop(6)
+    dqkv, wg, full, gown, gfar, dfirst, sums = pop(7)
     if ring:
         (gup,) = pop(1)
         dtok, oattn, oout, oup, ogain, oshift, obias, ohb, oqvb, oroot = pop(10)
@@ -924,7 +924,8 @@
         g = 0.0
         for j in range(4):
             g = g + mm(full[j, :, c], dqkv[j * rows : (j + 1) * rows, :], 0, 0)
-        gb[c, :] = jnp.concatenate([g.astype(BF), gout[c, :]], axis=1)
+        o = gown[c, :].astype(F32) + gfar[c, :].astype(F32)
+        gb[c, :] = jnp.concatenate([g, o], axis=1).astype(BF)
         return 0
 
     lax.fori_loop(0, d // 128, weight_part, 0)
@@ -1033,7 +1034,7 @@
     m1.wait_send()
 
 
-def last(n, ring, dqkv, wg, full, gout, dfirst, sums, gup):
+def last(n, ring, dqkv, wg, full, gown, gfar, dfirst, sums, gup):
     vm = pl.BlockSpec(memory_space=pltpu.VMEM)
     rows, d = dfirst.shape
     width = dqkv.shape[1] // 3
@@ -1041,7 +1042,7 @@
     nch = rows // ROWS
     s = jax.ShapeDtypeStruct
     V = pltpu.VMEM
-    ops = (dqkv, wg, full, gout, dfirst, sums)
+    ops = (dqkv, wg, full, gown, gfar, dfirst, sums)
     outs = [s((rows, d), F32)]
     gp = d // n
     k = DH // n
@@ -1194,8 +1195,7 @@
             hidden_bias.T,
             query_value_bias.transpose(1, 0, 2),
         )
-        got = project(n, tokens, width, segment_ids, padding, raw=raw)
-        wh, wd, wf = hidden_weight, down_weight.T, None
+        wh, wd, wg, wf = hidden_weight, down_weight.T, None, None
     else:
         gather = lambda x, dim: lax.all_gather(x, "fsdp", axis=dim, tiled=True)
         w = gather(attn_weight, 1).transpose(1, 0, 2).reshape(d, 3 * width)
@@ -1213,15 +1213,18 @@
             ]
         )
         wg = jnp.concatenate([jnp.concatenate([w, wo], axis=1), misc])[None]
-        got = project(n, tokens, width, segment_ids, padding, wg=wg)
         wf = jnp.concatenate([gather(hidden_weight, 0), gather(down_weight, 1).T], axis=1)[None]
-        wh = wd = None
-    full, qkv, misc, seg_row, seg_keys, pad_row, pad_cols, bounds, wg = got
-    layer_out, d_first, d_ctx, ctx_t, lse, g_out, g_hidden, g_down, sums = middle(
-        n, qkv, seg_row, seg_keys, pad_row, wg, misc, full, cotangent, pad_cols, wh, wd, wf
+        wh = wd = raw = None
+    got = list(
+        middle(n, tokens, cotangent, width, segment_ids, padding, raw, wh, wd, wg, wf)
     )
+    full, qkv, seg_row, seg_keys, pad_row, bounds = got[:6]
+    if ring:
+        wg = got.pop(6)
+    layer_out, d_first, d_ctx, ctx_t, lse, g_own, g_send, g_hidden, g_down, sums = got[6:]
+    g_far = lax.ppermute(g_send, "tensor", [(i, (i + 2) % 4) for i in range(4)])
     d_qkv = attn_bwd(bounds, qkv, d_ctx, ctx_t, lse, seg_row, seg_keys, pad_row)
-    done = last(n, ring, d_qkv, wg, full, g_out, d_first, sums, g_hidden)
+    done = last(n, ring, d_qkv, wg, full, g_own, g_far, d_first, sums, g_hidden)
     if ring:
         done = deliver((layer_out, g_down) + tuple(done[:-1]), done[-1])
         layer_out, g_down, d_tokens, g_attn, g_proj, g_hidden, g_gain, g_shift, g_bias, g_hb, g_qvb, roots = done

time: 197 us -> 186 us (0.944)
  Pallas kernels: 196 us -> 183 us
  starting transfers between devices: 0 us -> 2.43 us
    pallas_call x2 -> x1, Pallas kernels: 131 us -> 116 us  [middle(): pl.pallas_call(functools.partial(middle_kernel, n, ring), in_specs=specs,...]
    pallas_call x1, Pallas kernels: 21.3 us -> 24.6 us  [attn_bwd(): pl.pallas_call(functools.partial(bwd_kernel, heads), in_specs=[pl.BlockSp...]
    ppermute x0 -> x1, starting transfers between devices: none -> 2.43 us  [shards(): g_far = lax.ppermute(g_send, 'tensor', [(i, (i + 2) % 4) for i in range(4)])]
  transfers between devices with their start and end apart: 0 -> 1, of which waited for: 0 -> 0; matrix products, arithmetic and copies ran while one was open for 0% -> 0% of each run, Pallas kernels for 0% -> 13%
where the time goes in v1:
time: 186 us
  Pallas kernels  183 us (98%)
  starting transfers between devices  2.43 us (1%)
    pallas_call x1, Pallas kernels, middle(): pl.pallas_call(functools.partial(middle_kernel, n, ring), in_specs=specs,...  116 us
    pallas_call x1, Pallas kernels, last(): pl.pallas_call(functools.partial(last_kernel, n, ring), in_specs=[vm] * l...  39.8 us
    pallas_call x1, Pallas kernels, attn_bwd(): pl.pallas_call(functools.partial(bwd_kernel, heads), in_specs=[pl.BlockSp...  24.6 us
  transfers between devices with their start and end apart: 1, of which 0 were waited for; matrix products, arithmetic and copies ran while one was open for 0% of the time, Pallas kernels for 13%

profile of v1, /device:TPU:0, one launch (start us, length us, event | category | flops | bytes accessed | tf_op | source)
XLA Modules:
  0.0 185.9 jit_solution(16447016727791039313)
XLA Ops:
  0.6 116.1 %middle.1 = (bf16[4,384,768]{2,1,0:T(8,128)(2,1)S(1)}, bf16[3,1536,192]{2,1,0:T(8,128)(2,1)S(1)}, f32[1,1536]{1,0:T(1,128)S(1)}, f32[1536,128]{1,0:T(8,128)S(1)}...) custom-call(bf16[384,768]{1,0:T(8,128)(2,1)} %refs_0_.1, ...), custom_call_target="tpu_custom_call" | custom-call | tf_op jit(solution)/shard_map/middle/pallas_call | solution.py:866
  116.8 2.4 %collective-permute-start = (bf16[768,192]{1,0:T(8,128)(2,1)S(1)}, bf16[768,192]{1,0:T(8,128)(2,1)S(1)}, u32[]{:S(2)}, u32[]{:S(2)}) collective-permute-start(bf16[768,192]{1,0:T(8,128)(2,1)S(1)} %get-tuple-element.64), channel_id=1, source_target_pairs={{0,2},{1,3},{2,0},{3,1},{4,6},{5,7},{6,4},{7,5},{8,10},{9,11},{10,... | collective-permute-start | bytes 884744 | tf_op jit(solution)/shard_map/ppermute | solution.py:1225
  119.2 24.6 %attend_backward.1.refs_0_ = bf16[1536,576]{1,0:T(8,128)(2,1)S(1)} custom-call(s32[12]{0:T(128)S(1)} %get-tuple-element.53.bounds, bf16[3,1536,192]{2,1,0:T(8,128)(2,1)S(1)} %get-tuple-element.54.qkv_ref, bf16[1536,192]{1,0:T(8,128)(2,1)S(1)} %get-tuple-element.55.dc_ref, f32[192,1536]{1,0:T(8,128)S(1)} %get-tuple-element.56.oct_ref, ...), custom_call_target="tpu_custom_call" | custom-call | tf_op jit(solution)/shard_map/attend_backward/pallas_call | solution.py:1144
  143.8 0.0 collective-permute-done.refs_4_
  143.8 39.8 %last.1 = (f32[384,768]{1,0:T(8,128)S(1)}, f32[3,96,192]{2,1,0:T(8,128)S(1)}, f32[192,96]{1,0:T(8,128)S(1)}, f32[96,768]{1,0:T(8,128)S(1)}, f32[2,96]{1,0:T(2,12...) custom-call(bf16[1536,576]{1,0:T(8,128)(2,1)S(1)} %attend_backward.1, ...), custom_call_target="tpu_custom_call" | custom-call | tf_op jit(solution)/shard_map/last/pallas_call | solution.py:1062
  183.6 2.2 %deliver.1 = (bf16[384,768]{1,0:T(8,128)(2,1)}, f32[96,768]{1,0:T(8,128)}, f32[384,768]{1,0:T(8,128)}, f32[3,96,192]{2,1,0:T(8,128)}, f32[192,96]{1,0:T(8,128)},...) custom-call(bf16[384,768]{1,0:T(8,128)(2,1)S(1)} %get-tuple-element., ...), custom_call_target="tpu_custom_call" | custom-call | tf_op jit(solution)/shard_map/deliver/pallas_call | solution.py:1088
Async XLA Ops:
  116.8 27.0 %collective-permute-start = (bf16[768,192]{1,0:T(8,128)(2,1)S(1)}, bf16[768,192]{1,0:T(8,128)(2,1)S(1)}, u32[]{:S(2)}, u32[]{:S(2)}) collective-permute-start(bf16[768,192]{1,0:T(8,128)(2,1)S(1)} %get-tuple-element.64), channel_id=1, source_target_pairs={{0,2},{1,3},{2,0},{3,1},{4,6},{5,7},{6,4},{7,5},{8,10},{9,11},{10,... | collective-permute-start | bytes 884744 | tf_op jit(solution)/shard_map/ppermute | solution.py:1225

commit v2 on v1

--- a/solution.py
+++ b/solution.py
@@ -414,8 +414,7 @@
     full, qkv, sq, sk, live_row, bounds = pop(6)
     if ring:
         (wg,) = pop(1)
-    out, dfirst, dctx, octx, lse, gown, gsend, gup, odown, sums = pop(10)
-    gdown = odown
+    out, dfirst, dctx, octx, lse, gown, gsend, gup, gdown, sums = pop(10)
     misc, pad = pop(2)
     mine = near = nsem = psems = None
     if ring:
@@ -426,7 +425,7 @@
     if ring:
         psems = pop(4)
     if ring:
-        (wf, gdown) = pop(2)
+        (wf,) = pop(1)
     ctx, call, slab, wo, dsend = pop(5)
     (norm, dff, acted, dgelu, pre, dpre, first, xhat, r1, part, csem, lsem) = pop(12)
     cs, cr, xs, xr = pop(4)
@@ -440,7 +439,6 @@
     ff = wf.shape[2] // 2
     if ring:
         wsem = pop(4)
-        tracks = [pop(3) for _ in range(ff // 128)]
     t, f, core, cross, diag, place, at = places(n)
     rows, d = out.shape
     fetch = pltpu.make_async_copy(cot_hbm, out, csem.at[0])
@@ -760,28 +758,14 @@
             to[...] = (p + ocr[slot].astype(F32)).astype(BF)
 
     loop(feed_back)
-    if ring:
-        weight_part(dff, acted, gdown)
-        across(1, nch - 1)
-        go, close = ring_group(n, place, at, gdown, tracks)
-        go()
-        norm_one_back(0)
-        weight_part(norm, dpre, gup)
-        go()
-        for k in range(1, nch):
-            norm_one_back(k)
-            go()
-        out_part()
-        go()
-        out_take()
-        odown[...] = close()
-    else:
-        across(1, nch - 1)
-        weight_part(dff, acted, gdown)
-        weight_part(norm, dpre, gup)
-        loop(norm_one_back)
-        out_part()
-        out_take()
+    across(1, nch - 1)
+    weight_part(dff, acted, gdown)
+    norm_one_back(0)
+    weight_part(norm, dpre, gup)
+    for k in range(1, nch):
+        norm_one_back(k)
+    out_part()
+    out_take()
 
     def finish(k, _):
         end(1, k)
@@ -838,7 +822,7 @@
         s((d, width), BF),
         s((d, width), BF),
         s((d, ff), BF),
-        s((d // n, ff), F32) if ring else s((d, ff), BF),
+        s((d, ff), BF),
         s((8, d), F32),
     ]
     ospecs += [vm] * (len(outs) - len(ospecs))
@@ -851,7 +835,7 @@
     scratch += [DMA((2,))] + [DMA((nch,))] * 6
     if ring:
         scratch += [DMA((n // 2, 2))] * 4
-        scratch += [V((n, d // n, 2 * ff), BF), V((d, ff), BF)]
+        scratch += [V((n, d // n, 2 * ff), BF)]
     scratch += [V((total, width), BF), V((nch, 4, ROWS, width), BF), V((3, g, gr, wide), BF), V((4, d, width), BF)]
     scratch += [V((nch, 3, ROWS, width), BF)]
     scratch += [V((nch, 4, ROWS, d), BF)] * 2
@@ -862,7 +846,7 @@
     scratch += [V((2, d, width), BF)] * 2
     scratch += [DMA((2, nch))] * 10 + [DMA((1,))] * 8 + [DMA((nch,))] * 12
     if ring:
-        scratch += [DMA((n // 2, 2))] * 4 + ring_scratch(n, d // n, (128,) * (ff // 128))
+        scratch += [DMA((n // 2, 2))] * 4
     return pl.pallas_call(
         functools.partial(middle_kernel, n, ring),
         in_specs=specs,
@@ -876,15 +860,64 @@
     )(*ops)
 
 
+def attend_back_part(heads, reach, hook, qkv_ref, dc_ref, oct_ref, lse_ref, sq_ref, sk_ref, pad_ref, dqkv_ref, scratch):
+    qt, dt, kt, kh, vh, qh, dh, dqt, dsum, dka, dva = scratch
+    S=qkv_ref.shape[1]; W=heads*DH
+    qs=(qkv_ref[0].astype(F32)*0.125)
+    qsb=qs.astype(BF); qt[...]=qs.T.astype(BF)
+    kk=qkv_ref[1]; vv=qkv_ref[2]
+    kt[...]=kk.astype(F32).T.astype(BF)
+    dct=dc_ref[...].astype(F32).T*pad_ref[0:1,:]
+    dt[...]=dct.astype(BF)
+    dcn=dct.T.astype(BF)
+    prod=dct*oct_ref[...]
+    for h in range(heads):
+        c=slice(h*DH,(h+1)*DH)
+        kh[h]=kk[:,c]; vh[h]=vv[:,c]; qh[h]=qsb[:,c]; dh[h]=dcn[:,c]
+        dsum[h:h+1,:]=jnp.sum(prod[h*DH:(h+1)*DH],axis=0,keepdims=True)
+    dqt[...]=jnp.zeros_like(dqt)
+    def kblock(j):
+        k0=j*BK
+        lo=max(j-reach,0); hi=min(j+reach+1,S//BQ)
+        sk=jnp.concatenate([sk_ref[pl.ds(k0,BK),:]]*(BQ//128),axis=1)
+        kpos=k0+lax.broadcasted_iota(jnp.int32,(BK,BQ),0)
+        dka[...]=jnp.zeros_like(dka); dva[...]=jnp.zeros_like(dva)
+        def body(i,_):
+            q0=pl.multiple_of(i*BQ,BQ)
+            sq=sq_ref[0:1,pl.ds(q0,BQ)]
+            qpos=q0+lax.broadcasted_iota(jnp.int32,(BK,BQ),1)
+            ok=(sk==sq)|(kpos==qpos)
+            for h in range(heads):
+                r=slice(h*DH,(h+1)*DH)
+                s=jnp.where(ok,mm(kh[h,pl.ds(k0,BK),:],qt[r,pl.ds(q0,BQ)]),-1e30)
+                p=jnp.exp(s-lse_ref[h:h+1,pl.ds(q0,BQ)])
+                dp=mm(vh[h,pl.ds(k0,BK),:],dt[r,pl.ds(q0,BQ)])
+                ds=(p*(dp-dsum[h:h+1,pl.ds(q0,BQ)])).astype(BF)
+                dva[h]+=mm(p.astype(BF),dh[h,pl.ds(q0,BQ),:])
+                dka[h]+=mm(ds,qh[h,pl.ds(q0,BQ),:])
+                dqt[r,pl.ds(q0,BQ)]+=mm(kt[r,pl.ds(k0,BK)],ds)
+            return 0
+        lax.fori_loop(lo,hi,body,0)
+        dqkv_ref[pl.ds(k0,BK),W:]=jnp.concatenate([dka[h] for h in range(heads)]+[dva[h] for h in range(heads)],axis=1).astype(BF)
+    for j in range(S//BK):
+        kblock(j)
+        hook(j)
+    dqkv_ref[:,:W]=(dqt[...]*0.125).T.astype(BF)
+
+
 def last_kernel(n, ring, *refs):
     refs = list(refs)
     pop = lambda m: [refs.pop(0) for _ in range(m)]
-    dqkv, wg, full, gown, gfar, dfirst, sums = pop(7)
-    if ring:
-        (gup,) = pop(1)
-        dtok, oattn, oout, oup, ogain, oshift, obias, ohb, oqvb, oroot = pop(10)
+    qkv, dctx, octx, lse, sq, sk, live_row = pop(7)
+    wg, full, gown, gsend, dfirst, sums = pop(6)
+    if ring:
+        gup, gdown = pop(2)
+        dtok, oattn, oout, oup, odown, ogain, oshift, obias, ohb, oqvb, oroot = pop(11)
     else:
         dtok, gb, total = pop(3)
+    dqkv, gfar = pop(2)
+    bscratch = pop(11)
+    osem = pop(2)
     part, cs, cr, xs, xr = pop(5)
     rsem = pop(4)
     msend, mrecv = pop(2)
@@ -897,27 +930,42 @@
     rows, d = dtok.shape
     nch = rows // ROWS
     wpart = wg.shape[1] - MISC
-    w3 = dqkv.shape[1]
-    width = w3 // 3
+    width = qkv.shape[2]
+    w3 = 3 * width
     where = (t, core, cross, diag)
     put, across, take, end = scatter_tools(core, cross, part, cs, cr, xs, xr, rsem)
     nxt, prv = at((place + 1) % n), at((place + n - 1) % n)
 
     def rows_of(k):
         return pl.ds(pl.multiple_of(k * ROWS, ROWS), ROWS)
+
+    meet(core, cross, (nxt, prv) if ring else ())
+    ox = send(gsend, gfar, osem[0].at[0], osem[1].at[0], tensor=cross)
+    ox.start()
+    hooks = []
+    if ring:
+        ups, downs = gup.shape[1] // 128, gdown.shape[1] // 128
+        down, down_close = ring_group(n, place, at, gdown, tracks[:downs])
+        up, up_close = ring_group(n, place, at, gup, tracks[downs : downs + ups])
+        down()
+        up()
+        hooks = [down, up] * (n // 2)
+
+    def hook(j):
+        if j < len(hooks):
+            hooks[j]()
+
+    reach = (MOST - 2 + BK) // BK
+    attend_back_part(width // DH, reach, hook, qkv, dctx, octx, lse, sq, sk, live_row, dqkv, bscratch)
 
     b = col_sum(dqkv[...].astype(F32))
     b = jnp.concatenate([b[:, :width], b[:, 2 * width :], jnp.zeros((1, d - 2 * width), F32)], axis=1)
     msend[0] = sums[...]
     msend[0, 7:8, :] = sums[7:8, :] + b
-    meet(core, cross, (nxt, prv) if ring else ())
     m0 = send(msend.at[0], mrecv.at[0], msem[0].at[0], msem[1].at[0], tensor=core)
     m1 = send(msend.at[1], mrecv.at[1], msem[2].at[0], msem[3].at[0], tensor=cross)
-    if ring:
-        ups = gup.shape[1] // 128
-        up, up_close = ring_group(n, place, at, gup, tracks[:ups])
-        up()
     m0.start()
+    ox.wait_recv()
 
     def weight_part(i, _):
         c = pl.ds(pl.multiple_of(i * 128, 128), 128)
@@ -928,32 +976,24 @@
         gb[c, :] = jnp.concatenate([g, o], axis=1).astype(BF)
         return 0
 
-    lax.fori_loop(0, d // 128, weight_part, 0)
-    if ring:
-        up()
-        own, own_close = ring_group(n, place, at, gb, tracks[ups:])
-        own()
-
-        def go():
-            up()
-            own()
-
     def tokens_part(k):
         x = jnp.concatenate([dqkv[pl.ds(w * rows + k * ROWS, ROWS), :] for w in where], axis=0)
         put(0, k, lambda j: mm(x, some(wg, wpart, 0, w3, j, 2), 1, 1), 2)
 
-    for k in range(nch):
-        tokens_part(k)
-        if k > 0:
-            across(0, k - 1)
-        if ring and k > 0:
-            go()
-    across(0, nch - 1)
+    tokens_part(0)
+    lax.fori_loop(0, d // 256, weight_part, 0)
     m0.wait_recv()
     msend[1] = msend[0] + mrecv[0]
     m1.start()
-    if ring:
+    across(0, 0)
+    lax.fori_loop(d // 256, d // 128, weight_part, 0)
+    if ring:
+        go, own_close = ring_group(n, place, at, gb, tracks[ups + downs :])
         go()
+    for k in range(1, nch):
+        tokens_part(k)
+        if k > 1:
+            across(0, k - 1)
     m1.wait_recv()
     row = lax.broadcasted_iota(jnp.int32, (8, d), 0)
     col = lax.broadcasted_iota(jnp.int32, (8, d), 1)
@@ -976,18 +1016,26 @@
                 src = msend.at[2] if s == 0 else mall.at[b]
                 pair.append(send(src, mall.at[b], mring[2].at[s], mring[3].at[s], fsdp=prv))
             msteps.append(pair)
+        def spread(r):
+            for i, c in enumerate(msteps[r]):
+                if r > 0:
+                    msteps[r - 1][i].wait_recv()
+                c.start()
+
+        spread(0)
+        across(0, nch - 1)
+        go()
+        odown[...] = down_close()
         todo = [functools.partial(keep, k) for k in range(nch)]
-        r = 0
-        for _ in range(max(nch, far, n)):
-            if r < far:
-                for i, c in enumerate(msteps[r]):
-                    if r > 0:
-                        msteps[r - 1][i].wait_recv()
-                    c.start()
-                r += 1
+        for r in range(1, far):
+            spread(r)
             go()
+            if r == 1:
+                oup[...] = up_close()
             if todo:
                 todo.pop(0)()
+        for f_ in todo:
+            f_()
         msteps[far - 2][1].wait_recv()
         msteps[far - 1][0].wait_recv()
         total = jnp.sum(mall[...], axis=0)
@@ -1012,7 +1060,6 @@
         for j in range(3):
             o = jnp.where(col == j, jnp.sqrt(pick(j) / (count * d)), o)
         oroot[...] = o
-        oup[...] = up_close()
         x = own_close()
         for j in range(3):
             oattn[j] = x[:, j * width : (j + 1) * width]
@@ -1021,6 +1068,7 @@
             for c in pair:
                 c.wait_send()
     else:
+        across(0, nch - 1)
         total[...] = small
         for k in range(nch):
             keep(k)
@@ -1030,35 +1078,39 @@
         return 0
 
     lax.fori_loop(0, nch, finish, 0)
-    m0.wait_send()
-    m1.wait_send()
-
-
-def last(n, ring, dqkv, wg, full, gown, gfar, dfirst, sums, gup):
+    for c in (m0, m1, ox):
+        c.wait_send()
+
+
+def last(n, ring, qkv, dctx, octx, lse, sq, sk, live_row, wg, full, gown, gsend, dfirst, sums, gup, gdown):
     vm = pl.BlockSpec(memory_space=pltpu.VMEM)
     rows, d = dfirst.shape
-    width = dqkv.shape[1] // 3
+    width, total = qkv.shape[2], qkv.shape[1]
     heads = width // DH
     nch = rows // ROWS
     s = jax.ShapeDtypeStruct
     V = pltpu.VMEM
-    ops = (dqkv, wg, full, gown, gfar, dfirst, sums)
+    ops = (qkv, dctx, octx, lse, sq, sk, live_row, wg, full, gown, gsend, dfirst, sums)
     outs = [s((rows, d), F32)]
     gp = d // n
     k = DH // n
     if ring:
-        ops += (gup,)
-        outs += [s((3, gp, width), F32), s((width, gp), F32), s((gp, gup.shape[1]), F32)] + [s((2, gp), F32)] * 3
+        ops += (gup, gdown)
+        outs += [s((3, gp, width), F32), s((width, gp), F32), s((gp, gup.shape[1]), F32), s((gp, gdown.shape[1]), F32)] + [s((2, gp), F32)] * 3
         outs += [s((k, d // DH), F32), s((heads, 2, k), F32), s((1, 128), F32)]
     else:
         outs += [s((d, d), BF), s((8, d), F32)]
-    scratch = [V((nch, 2, ROWS, d), F32)]
+    scratch = [V((total, 3 * width), BF), V((d, width), BF)]
+    scratch += [V((width, total), BF)] * 3 + [V((heads, total, DH), BF)] * 4
+    scratch += [V((width, total), F32), V((heads, total), F32)] + [V((heads, BK, DH), F32)] * 2
+    scratch += [DMA((1,))] * 2
+    scratch += [V((nch, 2, ROWS, d), F32)]
     scratch += [V((nch, 2, ROWS, d), BF)] * 2 + [V((nch, ROWS, d), BF)] * 2
     scratch += [DMA((1, nch))] * 4
     scratch += [V((3, 8, d), F32), V((2, 8, d), F32)] + [DMA((1,))] * 4
     if ring:
         scratch += [V((d, d), BF), V((n, 8, d), F32)] + [DMA((n // 2,))] * 4
-        scratch += ring_scratch(n, gp, (128,) * ((gup.shape[1] + d) // 128))
+        scratch += ring_scratch(n, gp, (128,) * ((gup.shape[1] + gdown.shape[1] + d) // 128))
     return pl.pallas_call(
         functools.partial(last_kernel, n, ring),
         in_specs=[vm] * len(ops),
@@ -1066,7 +1118,7 @@
         out_shape=outs,
         scratch_shapes=scratch,
         compiler_params=pltpu.CompilerParams(
-            collective_id=3, has_side_effects=True, vmem_limit_bytes=12 << 20
+            collective_id=3, has_side_effects=True, vmem_limit_bytes=30 << 20
         ),
         name="last",
     )(*ops)
@@ -1094,60 +1146,6 @@
         compiler_params=pltpu.CompilerParams(vmem_limit_bytes=1 << 20),
         name="deliver",
     )(*arrays, roots)
-
-
-def bwd_kernel(heads, bounds, qkv_ref,dc_ref,oct_ref,lse_ref,sq_ref,sk_ref,pad_ref, dqkv_ref, qt, dt, kt, kh, vh, qh, dh, dqt, dsum, dka, dva):
-    S=qkv_ref.shape[1]; W=heads*DH
-    qs=(qkv_ref[0].astype(F32)*0.125)
-    qsb=qs.astype(BF); qt[...]=qs.T.astype(BF)
-    kk=qkv_ref[1]; vv=qkv_ref[2]
-    kt[...]=kk.astype(F32).T.astype(BF)
-    dct=dc_ref[...].astype(F32).T*pad_ref[0:1,:]
-    dt[...]=dct.astype(BF)
-    dcn=dct.T.astype(BF)
-    prod=dct*oct_ref[...]
-    for h in range(heads):
-        c=slice(h*DH,(h+1)*DH)
-        kh[h]=kk[:,c]; vh[h]=vv[:,c]; qh[h]=qsb[:,c]; dh[h]=dcn[:,c]
-        dsum[h:h+1,:]=jnp.sum(prod[h*DH:(h+1)*DH],axis=0,keepdims=True)
-    dqt[...]=jnp.zeros_like(dqt)
-    def kblock(j,_):
-        k0=pl.multiple_of(j*BK,BK)
-        lo=bounds[2*j]; hi=bounds[2*j+1]
-        sk=jnp.concatenate([sk_ref[pl.ds(k0,BK),:]]*(BQ//128),axis=1)
-        kpos=k0+lax.broadcasted_iota(jnp.int32,(BK,BQ),0)
-        dka[...]=jnp.zeros_like(dka); dva[...]=jnp.zeros_like(dva)
-        def body(i,_):
-            q0=pl.multiple_of(i*BQ,BQ)
-            sq=sq_ref[0:1,pl.ds(q0,BQ)]
-            qpos=q0+lax.broadcasted_iota(jnp.int32,(BK,BQ),1)
-            ok=(sk==sq)|(kpos==qpos)
-            for h in range(heads):
-                r=slice(h*DH,(h+1)*DH)
-                s=jnp.where(ok,mm(kh[h,pl.ds(k0,BK),:],qt[r,pl.ds(q0,BQ)]),-1e30)
-                p=jnp.exp(s-lse_ref[h:h+1,pl.ds(q0,BQ)])
-                dp=mm(vh[h,pl.ds(k0,BK),:],dt[r,pl.ds(q0,BQ)])
-                ds=(p*(dp-dsum[h:h+1,pl.ds(q0,BQ)])).astype(BF)
-                dva[h]+=mm(p.astype(BF),dh[h,pl.ds(q0,BQ),:])
-                dka[h]+=mm(ds,qh[h,pl.ds(q0,BQ),:])
-                dqt[r,pl.ds(q0,BQ)]+=mm(kt[r,pl.ds(k0,BK)],ds)
-            return 0
-        lax.fori_loop(lo,hi,body,0)
-        dqkv_ref[pl.ds(k0,BK),W:]=jnp.concatenate([dka[h] for h in range(heads)]+[dva[h] for h in range(heads)],axis=1).astype(BF)
-        return 0
-    lax.fori_loop(0,S//BK,kblock,0)
-    dqkv_ref[:,:W]=(dqt[...]*0.125).T.astype(BF)
-
-def attn_bwd(bounds,qkv,dc,oct,lse,sq,sk,pad):
-    _,S,W=qkv.shape; heads=W//DH
-    vm=pl.BlockSpec(memory_space=pltpu.VMEM)
-    return pl.pallas_call(functools.partial(bwd_kernel,heads),
-        in_specs=[pl.BlockSpec(memory_space=pltpu.SMEM)]+[vm]*7,
-        out_specs=vm,
-        out_shape=jax.ShapeDtypeStruct((S,3*W),BF),
-        scratch_shapes=[pltpu.VMEM((W,S),BF)]*3+[pltpu.VMEM((heads,S,DH),BF)]*4+[pltpu.VMEM((W,S),F32),pltpu.VMEM((heads,S),F32)]+[pltpu.VMEM((heads,BK,DH),F32)]*2,
-        compiler_params=pltpu.CompilerParams(vmem_limit_bytes=13<<20),
-        name="attend_backward")(bounds,qkv,dc,oct,lse,sq,sk,pad)
 
 
 def split_up(value, dim, devices):
@@ -1222,12 +1220,13 @@
     if ring:
         wg = got.pop(6)
     layer_out, d_first, d_ctx, ctx_t, lse, g_own, g_send, g_hidden, g_down, sums = got[6:]
-    g_far = lax.ppermute(g_send, "tensor", [(i, (i + 2) % 4) for i in range(4)])
-    d_qkv = attn_bwd(bounds, qkv, d_ctx, ctx_t, lse, seg_row, seg_keys, pad_row)
-    done = last(n, ring, d_qkv, wg, full, g_own, g_far, d_first, sums, g_hidden)
-    if ring:
-        done = deliver((layer_out, g_down) + tuple(done[:-1]), done[-1])
-        layer_out, g_down, d_tokens, g_attn, g_proj, g_hidden, g_gain, g_shift, g_bias, g_hb, g_qvb, roots = done
+    done = last(
+        n, ring, qkv, d_ctx, ctx_t, lse, seg_row, seg_keys, pad_row,
+        wg, full, g_own, g_send, d_first, sums, g_hidden, g_down,
+    )
+    if ring:
+        done = deliver((layer_out,) + tuple(done[:-1]), done[-1])
+        layer_out, d_tokens, g_attn, g_proj, g_hidden, g_down, g_gain, g_shift, g_bias, g_hb, g_qvb, roots = done
         g_down = g_down.T
         g_hb = g_hb.T
         g_qvb = g_qvb.transpose(1, 0, 2)

time: 186 us -> 173 us (0.930)
  Pallas kernels: 183 us -> 172 us
  starting transfers between devices: 2.43 us -> 0 us
    pallas_call x1 -> x0, Pallas kernels: 24.6 us -> none  [attn_bwd(): pl.pallas_call(functools.partial(bwd_kernel, heads), in_specs=[pl.BlockSp...]
    pallas_call x1, Pallas kernels: 39.8 us -> 55.9 us  [last(): pl.pallas_call(functools.partial(last_kernel, n, ring), in_specs=[vm] * l...]
    ppermute x1 -> x0, starting transfers between devices: 2.43 us -> none  [shards(): g_far = lax.ppermute(g_send, 'tensor', [(i, (i + 2) % 4) for i in range(4)])]
    pallas_call x1, Pallas kernels: 116 us -> 114 us  [middle(): pl.pallas_call(functools.partial(middle_kernel, n, ring), in_specs=specs,...]
  transfers between devices with their start and end apart: 1 -> 0, of which waited for: 0 -> 0; matrix products, arithmetic and copies ran while one was open for 0% -> 0% of each run, Pallas kernels for 13% -> 0%
where the time goes in v2:
time: 173 us
  Pallas kernels  172 us (99%)
    pallas_call x1, Pallas kernels, middle(): pl.pallas_call(functools.partial(middle_kernel, n, ring), in_specs=specs,...  114 us
    pallas_call x1, Pallas kernels, last(): pl.pallas_call(functools.partial(last_kernel, n, ring), in_specs=[vm] * l...  55.9 us

profile of v2, /device:TPU:0, one launch (start us, length us, event | category | flops | bytes accessed | tf_op | source)
XLA Modules:
  0.0 173.1 jit_solution(4824309821520492492)
XLA Ops:
  0.6 114.2 %middle.1 = (bf16[4,384,768]{2,1,0:T(8,128)(2,1)S(1)}, bf16[3,1536,192]{2,1,0:T(8,128)(2,1)S(1)}, f32[1,1536]{1,0:T(1,128)S(1)}, f32[1536,128]{1,0:T(8,128)S(1)}...) custom-call(bf16[384,768]{1,0:T(8,128)(2,1)} %refs_0_.1, ...), custom_call_target="tpu_custom_call" | custom-call | tf_op jit(solution)/shard_map/middle/pallas_call | solution.py:850
  114.8 55.9 %last.1 = (f32[384,768]{1,0:T(8,128)S(1)}, f32[3,96,192]{2,1,0:T(8,128)S(1)}, f32[192,96]{1,0:T(8,128)S(1)}, f32[96,768]{1,0:T(8,128)S(1)}, f32[96,768]{1,0:T(8,...) custom-call(bf16[3,1536,192]{2,1,0:T(8,128)(2,1)S(1)} %get-tuple-ele, ...), custom_call_target="tpu_custom_call" | custom-call | tf_op jit(solution)/shard_map/last/pallas_call | solution.py:1114
  170.7 2.2 %deliver.1 = (bf16[384,768]{1,0:T(8,128)(2,1)}, f32[384,768]{1,0:T(8,128)}, f32[3,96,192]{2,1,0:T(8,128)}, f32[192,96]{1,0:T(8,128)}, f32[96,768]{1,0:T(8,128)},...) custom-call(bf16[384,768]{1,0:T(8,128)(2,1)S(1)} %get-tuple-element., ...), custom_call_target="tpu_custom_call" | custom-call | tf_op jit(solution)/shard_map/deliver/pallas_call | solution.py:1140

commit v3 on v2

--- a/solution.py
+++ b/solution.py
@@ -264,6 +264,19 @@
             part[k, 1, :, c] = p[2 * m : 3 * m]
         a(i, k).start()
 
+    def put_half(i, k, b, tile, count):
+        if i > 0 and b == 0:
+            a(i - 1, k).wait_send()
+        width = part.shape[-1] // count
+        for j in range(count):
+            p = tile(j)
+            m = p.shape[0] // 2
+            c = slice(j * width, (j + 1) * width)
+            part[k, b, :, c] = p[:m]
+            cs[k, b, :, c] = p[m:].astype(BF)
+        if b == 1:
+            a(i, k).start()
+
     def across(i, k):
         a(i, k).wait_recv()
         if i > 0:
@@ -280,7 +293,7 @@
         a(i, k).wait_send()
         b(i, k).wait_send()
 
-    return put, across, take, end
+    return put, put_half, across, take, end
 
 
 def block_rows(ref, device, c0, c1, n):
@@ -449,7 +462,7 @@
     width = ctx.shape[1]
     heads = width // DH
     where = (t, core, cross, diag)
-    put, across, take, end = scatter_tools(core, cross, part, cs, cr, xs, xr, rsem)
+    put, put_half, across, take, end = scatter_tools(core, cross, part, cs, cr, xs, xr, rsem)
     gs = {}
     for i, buf in enumerate((norm, dff)):
         gs[i] = (
@@ -645,14 +658,22 @@
     inv = 0.7071067811865476
     thirds = ff // BQ
 
-    def feed(k):
-        shared(0, k)
-        def half(b):
-            x = norm[k, 2 * b : 2 * b + 2].reshape(2 * ROWS, d)
-            for c in range(0, ff, 256):
-                pre[:, c : c + 256] = mm(x, whole(wf, fpart, c, c + 256)) + misc[6:7, c : c + 256]
-
-        def act(i, b):
+    def far_rows(i, k):
+        gs[i][0](k).wait_recv()
+        gs[i][2](k).start()
+        if isinstance(k, int):
+            if k > 0:
+                across(i, k - 1)
+        else:
+            pl.when(k > 0)(lambda: across(i, k - 1))
+        gs[i][2](k).wait_recv()
+
+    def feed(k, b):
+        x = norm[k, 2 * b : 2 * b + 2].reshape(2 * ROWS, d)
+        for c in range(0, ff, 256):
+            pre[:, c : c + 256] = mm(x, whole(wf, fpart, c, c + 256)) + misc[6:7, c : c + 256]
+
+        def act(i, _):
             u = pre[pl.ds(pl.multiple_of(i * 64, 64), 64), :]
             s = pl.ds(pl.multiple_of(b * 2 * ROWS + i * 64, 64), 64)
             cdf = 0.5 + 0.5 * lax.erf(u * inv)
@@ -660,16 +681,25 @@
             slope = cdf + u * (jnp.exp(-0.5 * u * u) * 0.3989422804014327)
             for c in range(thirds):
                 dgelu[k * thirds + c, s, :] = slope[:, c * BQ : (c + 1) * BQ]
-            return b
-
-        half(0)
-        pl.when(k > 0)(lambda: across(0, k - 1))
+            return 0
+
         lax.fori_loop(0, 2 * ROWS // 64, act, 0)
-        half(1)
-        lax.fori_loop(0, 2 * ROWS // 64, act, 1)
-        put(0, k, lambda j: mm(acted[k], some(wf, fpart, ff, 2 * ff, j, 2), 1, 1), 2)
-
-    loop(feed)
+        y = acted[k, 2 * b * ROWS : 2 * (b + 1) * ROWS, :]
+        put_half(0, k, b, lambda j: mm(y, some(wf, fpart, ff, 2 * ff, j, 2), 1, 1), 2)
+
+    def feed_near(k):
+        gs[0][1](k).wait_recv()
+        feed(k, 0)
+
+    def feed_far(k):
+        far_rows(0, k)
+        feed(k, 1)
+
+    def feed_all(k):
+        feed_near(k)
+        feed_far(k)
+
+    loop(feed_all)
     across(0, nch - 1)
     fetch.wait()
 
@@ -690,28 +720,31 @@
 
     loop(norm_two)
 
-    def feed_back(k):
-        shared(1, k)
-        def half(b):
-            g = dff[k, 2 * b : 2 * b + 2].reshape(2 * ROWS, d)
-            for c in range(0, ff, 256):
-                pre[:, c : c + 256] = mm(g, whole(wf, fpart, ff + c, ff + c + 256))
-
-        def act(i, b):
+    def feed_back(k, b):
+        g = dff[k, 2 * b : 2 * b + 2].reshape(2 * ROWS, d)
+        for c in range(0, ff, 256):
+            pre[:, c : c + 256] = mm(g, whole(wf, fpart, ff + c, ff + c + 256))
+
+        def act(i, _):
             r = pl.ds(pl.multiple_of(i * 64, 64), 64)
             s = pl.ds(pl.multiple_of(b * 2 * ROWS + i * 64, 64), 64)
             slope = jnp.concatenate([dgelu[k * thirds + c, s, :] for c in range(thirds)], axis=1)
             low = (pre[r, :] * slope).astype(BF)
             dpre[k, s, :] = low
             sums[6:7, :] += col_sum(low.astype(F32))
-            return b
-
-        half(0)
-        pl.when(k > 0)(lambda: across(1, k - 1))
+            return 0
+
         lax.fori_loop(0, 2 * ROWS // 64, act, 0)
-        half(1)
-        lax.fori_loop(0, 2 * ROWS // 64, act, 1)
-        put(1, k, lambda j: mm(dpre[k], some(wf, fpart, 0, ff, j, 2), 1, 1), 2)
+        y = dpre[k, 2 * b * ROWS : 2 * (b + 1) * ROWS, :]
+        put_half(1, k, b, lambda j: mm(y, some(wf, fpart, 0, ff, j, 2), 1, 1), 2)
+
+    def back_near(k):
+        gs[1][1](k).wait_recv()
+        feed_back(k, 0)
+
+    def back_far(k):
+        far_rows(1, k)
+        feed_back(k, 1)
 
     def weight_part(left, right, to):
         def cols(i, _):
@@ -757,7 +790,13 @@
                 oc.wait_recv()
             to[...] = (p + ocr[slot].astype(F32)).astype(BF)
 
-    loop(feed_back)
+    for k in range(2):
+        back_near(k)
+    back_far(0)
+    for k in range(2, nch):
+        back_near(k)
+    for k in range(1, nch):
+        back_far(k)
     across(1, nch - 1)
     weight_part(dff, acted, gdown)
     norm_one_back(0)
@@ -933,7 +972,7 @@
     width = qkv.shape[2]
     w3 = 3 * width
     where = (t, core, cross, diag)
-    put, across, take, end = scatter_tools(core, cross, part, cs, cr, xs, xr, rsem)
+    put, put_half, across, take, end = scatter_tools(core, cross, part, cs, cr, xs, xr, rsem)
     nxt, prv = at((place + 1) % n), at((place + n - 1) % n)
 
     def rows_of(k):

time: 173 us -> 172 us (level)
    pallas_call x1, Pallas kernels: 114 us -> 112 us  [middle(): pl.pallas_call(functools.partial(middle_kernel, n, ring), in_specs=specs,...]
where the time goes in v3:
time: 172 us
  Pallas kernels  171 us (99%)
    pallas_call x1, Pallas kernels, middle(): pl.pallas_call(functools.partial(middle_kernel, n, ring), in_specs=specs,...  112 us
    pallas_call x1, Pallas kernels, last(): pl.pallas_call(functools.partial(last_kernel, n, ring), in_specs=[vm] * l...  57.1 us

profile of v3, /device:TPU:0, one launch (start us, length us, event | category | flops | bytes accessed | tf_op | source)
XLA Modules:
  0.0 172.1 jit_solution(446000998655181362)
XLA Ops:
  0.6 112.0 %middle.1 = (bf16[4,384,768]{2,1,0:T(8,128)(2,1)S(1)}, bf16[3,1536,192]{2,1,0:T(8,128)(2,1)S(1)}, f32[1,1536]{1,0:T(1,128)S(1)}, f32[1536,128]{1,0:T(8,128)S(1)}...) custom-call(bf16[384,768]{1,0:T(8,128)(2,1)} %refs_0_.1, ...), custom_call_target="tpu_custom_call" | custom-call | tf_op jit(solution)/shard_map/middle/pallas_call | solution.py:889
  112.6 57.1 %last.1 = (f32[384,768]{1,0:T(8,128)S(1)}, f32[3,96,192]{2,1,0:T(8,128)S(1)}, f32[192,96]{1,0:T(8,128)S(1)}, f32[96,768]{1,0:T(8,128)S(1)}, f32[96,768]{1,0:T(8,...) custom-call(bf16[3,1536,192]{2,1,0:T(8,128)(2,1)S(1)} %get-tuple-ele, ...), custom_call_target="tpu_custom_call" | custom-call | tf_op jit(solution)/shard_map/last/pallas_call | solution.py:1153
  169.8 2.2 %deliver.1 = (bf16[384,768]{1,0:T(8,128)(2,1)}, f32[384,768]{1,0:T(8,128)}, f32[3,96,192]{2,1,0:T(8,128)}, f32[192,96]{1,0:T(8,128)}, f32[96,768]{1,0:T(8,128)},...) custom-call(bf16[384,768]{1,0:T(8,128)(2,1)S(1)} %get-tuple-element., ...), custom_call_target="tpu_custom_call" | custom-call | tf_op jit(solution)/shard_map/deliver/pallas_call | solution.py:1179

commit v4 on v3

--- a/solution.py
+++ b/solution.py
@@ -799,10 +799,10 @@
         back_far(k)
     across(1, nch - 1)
     weight_part(dff, acted, gdown)
-    norm_one_back(0)
+    for k in range(nch - 1):
+        norm_one_back(k)
     weight_part(norm, dpre, gup)
-    for k in range(1, nch):
-        norm_one_back(k)
+    norm_one_back(nch - 1)
     out_part()
     out_take()
 

time: 172 us -> 172 us (level)
  no operation moved by 1% of the time
where the time goes in v4:
time: 172 us
  Pallas kernels  171 us (99%)
    pallas_call x1, Pallas kernels, middle(): pl.pallas_call(functools.partial(middle_kernel, n, ring), in_specs=specs,...  112 us
    pallas_call x1, Pallas kernels, last(): pl.pallas_call(functools.partial(last_kernel, n, ring), in_specs=[vm] * l...  57.2 us

profile of v4, /device:TPU:0, one launch (start us, length us, event | category | flops | bytes accessed | tf_op | source)
XLA Modules:
  0.0 172.1 jit_solution(1090488600280213566)
XLA Ops:
  0.6 111.9 %middle.1 = (bf16[4,384,768]{2,1,0:T(8,128)(2,1)S(1)}, bf16[3,1536,192]{2,1,0:T(8,128)(2,1)S(1)}, f32[1,1536]{1,0:T(1,128)S(1)}, f32[1536,128]{1,0:T(8,128)S(1)}...) custom-call(bf16[384,768]{1,0:T(8,128)(2,1)} %refs_0_.1, ...), custom_call_target="tpu_custom_call" | custom-call | tf_op jit(solution)/shard_map/middle/pallas_call | solution.py:889
  112.5 57.2 %last.1 = (f32[384,768]{1,0:T(8,128)S(1)}, f32[3,96,192]{2,1,0:T(8,128)S(1)}, f32[192,96]{1,0:T(8,128)S(1)}, f32[96,768]{1,0:T(8,128)S(1)}, f32[96,768]{1,0:T(8,...) custom-call(bf16[3,1536,192]{2,1,0:T(8,128)(2,1)S(1)} %get-tuple-ele, ...), custom_call_target="tpu_custom_call" | custom-call | tf_op jit(solution)/shard_map/last/pallas_call | solution.py:1153
  169.8 2.2 %deliver.1 = (bf16[384,768]{1,0:T(8,128)(2,1)}, f32[384,768]{1,0:T(8,128)}, f32[3,96,192]{2,1,0:T(8,128)}, f32[192,96]{1,0:T(8,128)}, f32[96,768]{1,0:T(8,128)},...) custom-call(bf16[384,768]{1,0:T(8,128)(2,1)S(1)} %get-tuple-element., ...), custom_call_target="tpu_custom_call" | custom-call | tf_op jit(solution)/shard_map/deliver/pallas_call | solution.py:1179
